TPU v7x, 32 devices: a whole 2x2x4 slice. The times are simulated.
32 devices in a mesh: pw: 8 (over z, x), band: 4 (over y, core).
Axes of the slice: x: 2, y: 2, z: 4, core: 2. Of those that a mesh axis runs over, the one named last changes fastest.
Arguments:
- basis_set: bfloat16 [24576, 2048], P('pw'), may hold values from -0.0546875 to 0.0546875
- densities: bfloat16 [24576, 4096], P('pw', 'band'), may hold values from -135 to 135
- pair_gaps: float32 [4096], P('band'), may hold values from 0.002 to 500
- frequencies: float32 [16], replicated, may hold values from 0.01 to 100
Outputs:
- polarizability: float32 [16, 2048, 2048], P(None, 'pw', 'band')
- projected: bfloat16 [2048, 4096], P('pw', 'band')
All inputs are finite; a program needn't handle non-finite values.
Results may differ from a plain program's by a relative error of at most 0.011.
Values may be sent and summed in bfloat16 or wider, within the bound.
No kernel may reach another device: no remote copies, remote signals or barrier semaphores. Data moves between devices by JAX's collectives and lax.ppermute only.
A program may use at most 128 MiB of HBM per device.

v0:
```python
import jax
import jax.numpy as jnp
from jax import lax
from jax.sharding import PartitionSpec as P

BATCH = 256
NBATCH = 4


def weigh(gap_row, frequencies, pair_total):
    return (
        -4.0 / pair_total * gap_row[None, :] / (gap_row[None, :] ** 2 + frequencies[:, None] ** 2)
    )


def scale_rows(weights, own_rows):
    return (weights[:, None, :] * own_rows.astype(jnp.float32)[None, :, :]).astype(jnp.bfloat16)


def on_device(basis_set, densities, pair_gaps, frequencies):
    basis_width = basis_set.shape[1]
    pw_count = lax.axis_size("pw")
    band_count = lax.axis_size("band")
    row_share = basis_width // pw_count
    pair_total = pair_gaps.shape[0] * band_count
    nfreq = frequencies.shape[0]
    accumulated = jnp.zeros((nfreq, row_share, basis_width // band_count), jnp.float32)
    all_gaps = lax.all_gather(pair_gaps.reshape(NBATCH, BATCH), "band", axis=1, tiled=True)
    collected = []
    for position in range(NBATCH):
        dens_block = densities[:, position * BATCH : (position + 1) * BATCH]
        own_rows = lax.psum_scatter(
            lax.dot_general(
                basis_set, dens_block, (((0,), (0,)), ((), ())), preferred_element_type=jnp.float32
            ),
            "pw",
            scatter_dimension=0,
            tiled=True,
        ).astype(jnp.bfloat16)
        gathered = lax.all_gather(own_rows, "pw", axis=0, tiled=True)
        collected.append(own_rows)
        columns = lax.all_to_all(gathered, "band", split_axis=0, concat_axis=1, tiled=True)
        rows_all = lax.all_gather(own_rows, "band", axis=1, tiled=True)
        scaled = scale_rows(weigh(all_gaps[position], frequencies, pair_total), rows_all)
        accumulated = accumulated + jnp.einsum(
            "krp,cp->krc", scaled, columns, preferred_element_type=jnp.float32
        )
    projected = jnp.concatenate(collected, axis=1)
    return (accumulated, projected)


def solution(mesh):
    in_specs = (P("pw", None), P("pw", "band"), P("band"), P())
    out_specs = (P(None, "pw", "band"), P("pw", "band"))
    return jax.shard_map(
        on_device, mesh=mesh, in_specs=in_specs, out_specs=out_specs, check_vma=False
    )
```

profile of v0, /device:TPU:0, one launch (start us, length us, event | category | flops | bytes accessed | tf_op | source)
XLA Modules:
  0.0 568.2 jit_solution(786625528526090730)
XLA Ops:
  7.2 10.0 %fusion.18 = f32[2048,256]{1,0:T(8,128)} fusion(bf16[3072,2048]{1,0:T(8,128)(2,1)} %param.4, bf16[3072,1024]{1,0:T(8,128)(2,1)} %param.5), kind=kOutput, calls=%fused_computation.23 | convolution fusion | flops 3221225472 | bytes 16252928 | tf_op jit(solution)/shard_map/dot_general | solution.py:33
  17.2 0.0 reduce-scatter.7.cloned.1.call-start
  17.3 10.0 %fusion.16 = f32[2048,256]{1,0:T(8,128)} fusion(bf16[3072,2048]{1,0:T(8,128)(2,1)} %param.4, bf16[3072,1024]{1,0:T(8,128)(2,1)} %param.5), kind=kOutput, calls=%fused_computation.21 | convolution fusion | flops 3221225472 | bytes 16252928 | tf_op jit(solution)/shard_map/dot_general | solution.py:33
  27.3 0.0 reduce-scatter.9.cloned.1.call-start
  27.4 10.0 %fusion.14 = f32[2048,256]{1,0:T(8,128)} fusion(bf16[3072,2048]{1,0:T(8,128)(2,1)} %param.4, bf16[3072,1024]{1,0:T(8,128)(2,1)} %param.5), kind=kOutput, calls=%fused_computation.19 | convolution fusion | flops 3221225472 | bytes 16252928 | tf_op jit(solution)/shard_map/dot_general | solution.py:33
  37.4 0.0 all-gather.5.cloned.1.call-start
  37.4 51.0 %reduce-scatter.5.cloned.1.call-done = f32[256,256]{1,0:T(8,128)} async-done(((f32[2048,256]{1,0:T(8,128)}), f32[256,256]{1,0:T(8,128)}) %reduce-scatter.5.cloned.1.call-update) | async-done | bytes 262160 | tf_op jit(solution)/shard_map/reduce_scatter | solution.py:32
  88.4 1.6 convert_element_type.36
  90.1 0.2 reduce-scatter.11.cloned.1.call-start
  90.3 10.0 %fusion.12 = f32[2048,256]{1,0:T(8,128)} fusion(bf16[3072,2048]{1,0:T(8,128)(2,1)} %param.4, bf16[3072,1024]{1,0:T(8,128)(2,1)} %param.5), kind=kOutput, calls=%fused_computation.17 | convolution fusion | flops 3221225472 | bytes 16252928 | tf_op jit(solution)/shard_map/dot_general | solution.py:33
  100.3 0.0 all-gather.7.cloned.1.call-start
  100.4 59.0 %reduce-scatter.7.cloned.1.call-done = f32[256,256]{1,0:T(8,128)} async-done(((f32[2048,256]{1,0:T(8,128)}), f32[256,256]{1,0:T(8,128)}) %reduce-scatter.7.cloned.1.call-update) | async-done | bytes 262160 | tf_op jit(solution)/shard_map/reduce_scatter | solution.py:32
  159.3 1.6 convert_element_type.39
  161.0 70.0 %reduce-scatter.9.cloned.1.call-done = f32[256,256]{1,0:T(8,128)} async-done(((f32[2048,256]{1,0:T(8,128)}), f32[256,256]{1,0:T(8,128)}) %reduce-scatter.9.cloned.1.call-update) | async-done | bytes 262160 | tf_op jit(solution)/shard_map/reduce_scatter | solution.py:32
  231.0 1.6 convert_element_type.42
  232.6 39.5 %all-gather.5.cloned.1.call-done = bf16[2048,256]{1,0:T(8,128)(2,1)} async-done(((bf16[256,256]{1,0:T(8,128)(2,1)}), bf16[2048,256]{1,0:T(8,128)(2,1)}) %all-gather.5.cloned.1.call-update) | async-done | bytes 1048592 | tf_op jit(solution)/shard_map/all_gather | solution.py:40
  272.1 3.5 all-to-all-start
  275.7 67.0 %reduce-scatter.11.cloned.1.call-done = f32[256,256]{1,0:T(8,128)} async-done(((f32[2048,256]{1,0:T(8,128)}), f32[256,256]{1,0:T(8,128)}) %reduce-scatter.11.cloned.1.call-update) | async-done | bytes 262160 | tf_op jit(solution)/shard_map/reduce_scatter | solution.py:32
  342.7 1.6 convert_element_type.45
  344.3 39.7 %all-gather.7.cloned.1.call-done = bf16[2048,256]{1,0:T(8,128)(2,1)} async-done(((bf16[256,256]{1,0:T(8,128)(2,1)}), bf16[2048,256]{1,0:T(8,128)(2,1)}) %all-gather.7.cloned.1.call-update) | async-done | bytes 1048592 | tf_op jit(solution)/shard_map/all_gather | solution.py:40
  384.0 3.5 all-to-all-start.1
  387.6 38.2 %all-gather.9.cloned.1.call-done = bf16[2048,256]{1,0:T(8,128)(2,1)} async-done(((bf16[256,256]{1,0:T(8,128)(2,1)}), bf16[2048,256]{1,0:T(8,128)(2,1)}) %all-gather.9.cloned.1.call-update) | async-done | bytes 1048592 | tf_op jit(solution)/shard_map/all_gather | solution.py:40
  425.8 3.5 all-to-all-start.2
  429.3 15.4 %all_gather.27 = f32[4,1024]{1,0:T(4,128)S(1)} all-gather(f32[4,256]{1,0:T(4,128)S(1)} %reshape.166), channel_id=1, replica_groups=mesh['pw'=8,'band'=4] {'band'}, dimensions={1}, use_global_device_ids=true | all-gather | bytes 20480 | tf_op jit(solution)/shard_map/all_gather | solution.py:28
  444.7 0.8 add_divide_fusion
  445.5 21.4 %all-gather.11.cloned.1.call-done = bf16[2048,256]{1,0:T(8,128)(2,1)} async-done(((bf16[256,256]{1,0:T(8,128)(2,1)}), bf16[2048,256]{1,0:T(8,128)(2,1)}) %all-gather.11.cloned.1.call-update) | async-done | bytes 1048592 | tf_op jit(solution)/shard_map/all_gather | solution.py:40
  466.9 4.2 all-to-all-start.3
  471.2 18.0 %all_gather.28 = bf16[256,1024]{1,0:T(8,128)(2,1)S(1)} all-gather(bf16[256,256]{1,0:T(8,128)(2,1)S(1)} %copy-done), channel_id=1, replica_groups=mesh['pw'=8,'band'=4] {'band'}, dimensions={1}, use_global_device_ids=true | all-gather | bytes 655360 | tf_op jit(solution)/shard_map/all_gather | solution.py:43
  489.2 1.1 convert_element_type.37
  490.3 7.3 %all_gather.30 = bf16[256,1024]{1,0:T(8,128)(2,1)S(1)} all-gather(bf16[256,256]{1,0:T(8,128)(2,1)S(1)} %copy-done.1), channel_id=1, replica_groups=mesh['pw'=8,'band'=4] {'band'}, dimensions={1}, use_global_device_ids=true | all-gather | bytes 655360 | tf_op jit(solution)/shard_map/all_gather | solution.py:43
  497.6 1.1 convert_element_type.40
  498.7 7.3 %all_gather.32 = bf16[256,1024]{1,0:T(8,128)(2,1)S(1)} all-gather(bf16[256,256]{1,0:T(8,128)(2,1)S(1)} %copy-done.2), channel_id=1, replica_groups=mesh['pw'=8,'band'=4] {'band'}, dimensions={1}, use_global_device_ids=true | all-gather | bytes 655360 | tf_op jit(solution)/shard_map/all_gather | solution.py:43
  505.9 1.1 convert_element_type.43
  507.0 7.5 %all_gather.34 = bf16[256,1024]{1,0:T(8,128)(2,1)S(1)} all-gather(bf16[256,256]{1,0:T(8,128)(2,1)} %convert_element_type.45), channel_id=1, replica_groups=mesh['pw'=8,'band'=4] {'band'}, dimensions={1}, use_global_device_ids=true | all-gather | bytes 655360 | tf_op jit(solution)/shard_map/all_gather | solution.py:43
  514.5 1.1 convert_element_type.46
  515.6 0.9 pad_maximum_fusion
  516.5 1.8 copy.6
  518.3 2.6 reshape.167
  520.9 0.8 copy.7
  521.7 1.6 reshape.168
  523.3 0.8 copy.8
  524.1 0.8 reshape.169
  524.9 2.0 copy.9
  526.9 1.6 reshape.170
  528.5 7.9 %fusion = f32[16,256,512]{2,1,0:T(8,128)} fusion(bf16[512,1024,1]{1,0,2:T(8,128)(2,1)S(1)} %copy-done.7, f32[256,1024]{1,0:T(8,128)} %convert_element_type.37, f32[16,1024]{1,0:T(8,128)} %get-tuple-element.13), kind=kOutput, calls=%fused_computation.4 | convolution fusion | flops 4303355904 | bytes 10551296 | tf_op jit(solution)/shard_map/krp,cp->krc/dot_general | solution.py:45
  536.5 6.8 %fusion.1 = f32[16,256,512]{2,1,0:T(8,128)} fusion(bf16[512,1024,1]{1,0,2:T(8,128)(2,1)S(1)} %copy-done.8, f32[256,1024]{1,0:T(8,128)S(1)} %copy-done.6, f32[16,1024]{1,0:T(8,128)S(1)} %copy-done.12), kind=kOutput, calls=%fused_computation.5 | convolution fusion | flops 4303355904 | bytes 10551296 | tf_op jit(solution)/shard_map/krp,cp->krc/dot_general | solution.py:45
  543.3 6.8 %fusion.2 = f32[16,256,512]{2,1,0:T(8,128)} fusion(bf16[512,1024,1]{1,0,2:T(8,128)(2,1)S(1)} %reshape.169, f32[256,1024]{1,0:T(8,128)S(1)} %copy-done.5, f32[16,1024]{1,0:T(8,128)S(1)} %copy-done.11), kind=kOutput, calls=%fused_computation.6 | convolution fusion | flops 4303355904 | bytes 10551296 | tf_op jit(solution)/shard_map/krp,cp->krc/dot_general | solution.py:45
  550.1 11.2 %add_add_fusion = f32[16,256,512]{2,1,0:T(8,128)} fusion(f32[16,256,512]{2,1,0:T(8,128)} %fusion.2, f32[16,256,512]{2,1,0:T(8,128)S(1)} %bitcast.40, f32[16,256,512]{2,1,0:T(8,128)} %fusion.1, bf16[512,1024,1]{1,0,2:T(8,128)(2,1)S(1)} %copy-done.9, f32[256,1024]{1,0:T(8,128)S(1)} %copy-done.4, f32[16,1024]{1,0:T(8,128)S(1)} %copy-done.10), kind=kOutput, calls=%fused_computation.10 | convolution fusion | flops 4309647360 | bytes 35717120 | tf_op jit(solution)/shard_map/krp,cp->krc/dot_general | solution.py:45
  (53 shorter events, 0.4 us)
Async XLA Ops:
  7.2 81.3 %reduce-scatter.5.cloned.1.call-start = ((), (), s32[]{:S(2)}) async-start(), calls=%async_computation.8 | async-start | bytes 2359296 | tf_op jit(solution)/shard_map/reduce_scatter | solution.py:32
  17.2 142.1 %reduce-scatter.7.cloned.1.call-start = ((), (), s32[]{:S(2)}) async-start(), calls=%async_computation.10 | async-start | bytes 2359296 | tf_op jit(solution)/shard_map/reduce_scatter | solution.py:32
  27.3 203.7 %reduce-scatter.9.cloned.1.call-start = ((), (), s32[]{:S(2)}) async-start(), calls=%async_computation.12 | async-start | bytes 2359296 | tf_op jit(solution)/shard_map/reduce_scatter | solution.py:32
  37.4 234.8 %all-gather.5.cloned.1.call-start = ((), (), s32[]{:S(2)}) async-start(), calls=%async_computation.9 | async-start | bytes 1179648 | tf_op jit(solution)/shard_map/all_gather | solution.py:40
  90.1 252.6 %reduce-scatter.11.cloned.1.call-start = ((), (), s32[]{:S(2)}) async-start(), calls=%async_computation.14 | async-start | bytes 2359296 | tf_op jit(solution)/shard_map/reduce_scatter | solution.py:32
  100.3 329.0 %copy-start.13 = (f32[1024]{0:T(1024)S(1)}, f32[1024]{0:T(1024)}, u32[]{:S(2)}) copy-start(f32[1024]{0:T(1024)} %param.6) | copy-start | bytes 12292
  100.3 329.0 %copy-start.14 = (f32[16]{0:T(128)S(1)}, f32[16]{0:T(128)}, u32[]{:S(2)}) copy-start(f32[16]{0:T(128)} %param.7) | copy-start | bytes 196
  100.3 370.8 %copy-start = (bf16[256,256]{1,0:T(8,128)(2,1)S(1)}, bf16[256,256]{1,0:T(8,128)(2,1)}, u32[]{:S(2)}) copy-start(bf16[256,256]{1,0:T(8,128)(2,1)} %convert_element_type.36) | copy-start | bytes 393220
  100.3 283.7 %all-gather.7.cloned.1.call-start = ((), (), s32[]{:S(2)}) async-start(), calls=%async_computation.11 | async-start | bytes 1179648 | tf_op jit(solution)/shard_map/all_gather | solution.py:40
  161.0 329.3 %copy-start.1 = (bf16[256,256]{1,0:T(8,128)(2,1)S(1)}, bf16[256,256]{1,0:T(8,128)(2,1)}, u32[]{:S(2)}) copy-start(bf16[256,256]{1,0:T(8,128)(2,1)} %convert_element_type.39) | copy-start | bytes 393220
  161.0 264.8 %all-gather.9.cloned.1.call-start = ((), (), s32[]{:S(2)}) async-start(), calls=%async_computation.13 | async-start | bytes 1179648 | tf_op jit(solution)/shard_map/all_gather | solution.py:40
  232.6 266.1 %copy-start.2 = (bf16[256,256]{1,0:T(8,128)(2,1)S(1)}, bf16[256,256]{1,0:T(8,128)(2,1)}, u32[]{:S(2)}) copy-start(bf16[256,256]{1,0:T(8,128)(2,1)} %convert_element_type.42) | copy-start | bytes 393220
  272.1 111.9 %all-to-all-start = ((bf16[4,512,256]{2,1,0:T(8,128)(2,1)}), bf16[4,512,256]{2,1,0:T(8,128)(2,1)S(1)}, u32[]{:S(2)}, u32[]{:S(2)}) async-start(bf16[4,512,256]{2,1,0:T(8,128)(2,1)} %bitcast.29), calls=%async_computation.1 | async-start | bytes 2097152 | tf_op jit(solution)/shard_map/all_to_all | solution.py:42
  275.7 191.2 %all-gather.11.cloned.1.call-start = ((), (), s32[]{:S(2)}) async-start(), calls=%async_computation.15 | async-start | bytes 1179648 | tf_op jit(solution)/shard_map/all_gather | solution.py:40
  384.0 41.7 %all-to-all-start.1 = ((bf16[4,512,256]{2,1,0:T(8,128)(2,1)}), bf16[4,512,256]{2,1,0:T(8,128)(2,1)S(1)}, u32[]{:S(2)}, u32[]{:S(2)}) async-start(bf16[4,512,256]{2,1,0:T(8,128)(2,1)} %bitcast.30), calls=%async_computation.3 | async-start | bytes 2097152 | tf_op jit(solution)/shard_map/all_to_all | solution.py:42
  425.8 41.1 %all-to-all-start.2 = ((bf16[4,512,256]{2,1,0:T(8,128)(2,1)}), bf16[4,512,256]{2,1,0:T(8,128)(2,1)S(1)}, u32[]{:S(2)}, u32[]{:S(2)}) async-start(bf16[4,512,256]{2,1,0:T(8,128)(2,1)} %bitcast.28), calls=%async_computation.5 | async-start | bytes 2097152 | tf_op jit(solution)/shard_map/all_to_all | solution.py:42
  466.9 58.0 %all-to-all-start.3 = ((bf16[4,512,256]{2,1,0:T(8,128)(2,1)}), bf16[4,512,256]{2,1,0:T(8,128)(2,1)}, u32[]{:S(2)}, u32[]{:S(2)}) async-start(bf16[4,512,256]{2,1,0:T(8,128)(2,1)} %bitcast.27), calls=%async_computation.7 | async-start | bytes 2097152 | tf_op jit(solution)/shard_map/all_to_all | solution.py:42
  471.2 44.5 %copy-start.3 = (bf16[256,256]{1,0:T(8,128)(2,1)S(1)}, bf16[256,256]{1,0:T(8,128)(2,1)}, u32[]{:S(2)}) copy-start(bf16[256,256]{1,0:T(8,128)(2,1)} %convert_element_type.45) | copy-start | bytes 393220
  521.7 6.8 %copy-start.7 = (bf16[512,1024,1]{1,0,2:T(8,128)(2,1)S(1)}, bf16[512,1024,1]{1,0,2:T(8,128)(2,1)}, u32[]{:S(2)}) copy-start(bf16[512,1024,1]{1,0,2:T(8,128)(2,1)} %reshape.167) | copy-start | bytes 3145732
  528.5 8.0 %copy-start.6 = (f32[256,1024]{1,0:T(8,128)S(1)}, f32[256,1024]{1,0:T(8,128)}, u32[]{:S(2)}) copy-start(f32[256,1024]{1,0:T(8,128)} %convert_element_type.40) | copy-start | bytes 3145732
  528.5 8.0 %copy-start.8 = (bf16[512,1024,1]{1,0,2:T(8,128)(2,1)S(1)}, bf16[512,1024,1]{1,0,2:T(8,128)(2,1)}, u32[]{:S(2)}) copy-start(bf16[512,1024,1]{1,0,2:T(8,128)(2,1)} %reshape.168) | copy-start | bytes 3145732
  528.5 8.0 %copy-start.12 = (f32[16,1024]{1,0:T(8,128)S(1)}, f32[16,1024]{1,0:T(8,128)}, u32[]{:S(2)}) copy-start(f32[16,1024]{1,0:T(8,128)} %get-tuple-element.11) | copy-start | bytes 196612
  536.4 6.8 %copy-start.5 = (f32[256,1024]{1,0:T(8,128)S(1)}, f32[256,1024]{1,0:T(8,128)}, u32[]{:S(2)}) copy-start(f32[256,1024]{1,0:T(8,128)} %convert_element_type.43) | copy-start | bytes 3145732
  536.4 6.8 %copy-start.11 = (f32[16,1024]{1,0:T(8,128)S(1)}, f32[16,1024]{1,0:T(8,128)}, u32[]{:S(2)}) copy-start(f32[16,1024]{1,0:T(8,128)} %get-tuple-element.12) | copy-start | bytes 196612
  536.5 13.6 %slice-start = ((s8[8388608]{0:T(1024)(128)(4,1)}), s8[4194304]{0:T(1024)(128)(4,1)S(1)}, s32[]{:S(2)}) async-start(s8[8388608]{0:T(1024)(128)(4,1)} %bitcast.39), calls=%async_computation.16 | async-start | bytes 8388608
  543.3 6.8 %copy-start.4 = (f32[256,1024]{1,0:T(8,128)S(1)}, f32[256,1024]{1,0:T(8,128)}, u32[]{:S(2)}) copy-start(f32[256,1024]{1,0:T(8,128)} %convert_element_type.46) | copy-start | bytes 3145732
  543.3 6.8 %copy-start.9 = (bf16[512,1024,1]{1,0,2:T(8,128)(2,1)S(1)}, bf16[512,1024,1]{1,0,2:T(8,128)(2,1)}, u32[]{:S(2)}) copy-start(bf16[512,1024,1]{1,0,2:T(8,128)(2,1)} %reshape.170) | copy-start | bytes 3145732
  543.3 6.8 %copy-start.10 = (f32[16,1024]{1,0:T(8,128)S(1)}, f32[16,1024]{1,0:T(8,128)}, u32[]{:S(2)}) copy-start(f32[16,1024]{1,0:T(8,128)} %get-tuple-element.10) | copy-start | bytes 196612
  543.3 6.8 %slice-start.1 = ((s8[8388608]{0:T(1024)(128)(4,1)}), s8[4194304]{0:T(1024)(128)(4,1)S(1)}, s32[]{:S(2)}) async-start(s8[8388608]{0:T(1024)(128)(4,1)} %bitcast.39), calls=%async_computation.17 | async-start | bytes 8388608
Sparse Core Ops, SparseCore 0:
  17.4 71.0 reduce-scatter.4
  92.0 67.3 reduce-scatter.6
  163.5 67.4 reduce-scatter.8
  233.0 39.1 all-gather.4
  275.5 67.1 reduce-scatter.10
  344.7 39.3 all-gather.6
  386.7 38.9 all-gather.8
  427.9 38.9 all-gather.10
where the time goes:
time: 569 us; the launch traced here: 568 us
  waiting for transfers between devices  386 us (68%)
  matrix products  72.8 us (13%)
  blocking collectives  55.4 us (10%)
  starting transfers between devices  15.3 us (3%)
  between operations  14.3 us (3%)
  other arithmetic  12.5 us (2%)
  local copies, waits for them, and re-layouts  12 us (2%)
    reduce_scatter x4, waiting for transfers between devices, on_device(): lax.psum_scatter(lax.dot_general(basis_set, dens_block, (((0,), (0,)), ((...  247 us
    all_gather x4, waiting for transfers between devices, on_device(): gathered = lax.all_gather(own_rows, 'pw', axis=0, tiled=True)  139 us
    all_gather x4, blocking collectives, on_device(): rows_all = lax.all_gather(own_rows, 'band', axis=1, tiled=True)  40 us
    dot_general x4, matrix products, on_device(): lax.dot_general(basis_set, dens_block, (((0,), (0,)), ((), ())), preferre...  40 us
    dot_general x4, matrix products, on_device(): jnp.einsum('krp,cp->krc', scaled, columns, preferred_element_type=jnp.flo...  32.8 us
    all_gather x1, blocking collectives, on_device(): lax.all_gather(pair_gaps.reshape(NBATCH, BATCH), 'band', axis=1, tiled=True)  15.4 us
    all_to_all x4, starting transfers between devices, on_device(): lax.all_to_all(gathered, 'band', split_axis=0, concat_axis=1, tiled=True)  14.8 us
    all_to_all x8, local copies, waits for them, and re-layouts, on_device(): lax.all_to_all(gathered, 'band', split_axis=0, concat_axis=1, tiled=True)  11.9 us
  transfers between devices with their start and end apart: 12, of which 8 were waited for; matrix products, arithmetic and copies ran while one was open for 9% of the time, Pallas kernels for 0%

commit v1 on v0

--- a/solution.py
+++ b/solution.py
@@ -1,10 +1,16 @@
+import functools
+
 import jax
 import jax.numpy as jnp
 from jax import lax
+from jax.experimental import pallas as pl
+from jax.experimental.pallas import tpu as pltpu
 from jax.sharding import PartitionSpec as P
 
 BATCH = 256
 NBATCH = 4
+AXES = ("pw", "band")
+VMEM = pl.BlockSpec(memory_space=pltpu.VMEM)
 
 
 def weigh(gap_row, frequencies, pair_total):
@@ -17,7 +23,7 @@
     return (weights[:, None, :] * own_rows.astype(jnp.float32)[None, :, :]).astype(jnp.bfloat16)
 
 
-def on_device(basis_set, densities, pair_gaps, frequencies):
+def plain_on_device(basis_set, densities, pair_gaps, frequencies):
     basis_width = basis_set.shape[1]
     pw_count = lax.axis_size("pw")
     band_count = lax.axis_size("band")
@@ -49,9 +55,272 @@
     return (accumulated, projected)
 
 
+def project_kernel(me, dens_ref, basis_ref, *outs):
+    step = pl.program_id(0)
+    part = lax.dot_general(
+        basis_ref[...],
+        dens_ref[...],
+        (((0,), (0,)), ((), ())),
+        preferred_element_type=jnp.float32,
+    ).astype(jnp.bfloat16)
+    width = outs[0].shape[2]
+    for i, out in enumerate(outs):
+        out[step] = part[:, i * width : (i + 1) * width]
+
+
+def project(me, basis_set, densities, block, count, width, planes, rows, own):
+    depth = basis_set.shape[0]
+
+    def basis_at(step, me):
+        mine = jnp.bitwise_xor(me[0], step * 2)
+        return (0, mine if own else jnp.bitwise_xor(mine, 1))
+
+    return pl.pallas_call(
+        project_kernel,
+        grid_spec=pltpu.PrefetchScalarGridSpec(
+            num_scalar_prefetch=1,
+            grid=(planes,),
+            in_specs=[
+                pl.BlockSpec((depth, count * width), lambda step, me: (0, block)),
+                pl.BlockSpec((depth, rows), basis_at),
+            ],
+            out_specs=[VMEM] * count,
+        ),
+        out_shape=[jax.ShapeDtypeStruct((planes, rows, width), jnp.bfloat16)] * count,
+        cost_estimate=pl.CostEstimate(
+            flops=2 * depth * count * width * rows * planes,
+            bytes_accessed=2 * depth * (count * width + rows * planes),
+            transcendentals=0,
+        ),
+        compiler_params=pltpu.CompilerParams(
+            dimension_semantics=("arbitrary",), vmem_limit_bytes=28 << 20
+        ),
+        name="project",
+    )(me, densities, basis_set)
+
+
+def fold_kernel(kept_ref, got_ref, *outs):
+    for i in range(kept_ref.shape[0]):
+        total = (kept_ref[i].astype(jnp.float32) + got_ref[i].astype(jnp.float32)).astype(
+            jnp.bfloat16
+        )
+        if kept_ref.shape[0] == 1:
+            outs[0][...] = total
+        else:
+            outs[i % 2][i // 2] = total
+
+
+def fold(kept, got):
+    count, rows, width = kept.shape
+    if count == 1:
+        shapes = [jax.ShapeDtypeStruct((rows, width), jnp.bfloat16)]
+    else:
+        shapes = [jax.ShapeDtypeStruct((count // 2, rows, width), jnp.bfloat16)] * 2
+    return pl.pallas_call(
+        fold_kernel,
+        in_specs=[VMEM] * 2,
+        out_specs=[VMEM] * len(shapes),
+        out_shape=shapes,
+        cost_estimate=pl.CostEstimate(
+            flops=count * rows * width, bytes_accessed=4 * count * rows * width, transcendentals=0
+        ),
+        compiler_params=pltpu.CompilerParams(vmem_limit_bytes=8 << 20),
+        name="fold",
+    )(kept, got)
+
+
+def stack_kernel(*refs):
+    for i, ref in enumerate(refs[:-1]):
+        refs[-1][i] = ref[...]
+
+
+def stack(pieces):
+    rows, width = pieces[0].shape
+    return pl.pallas_call(
+        stack_kernel,
+        in_specs=[VMEM] * len(pieces),
+        out_specs=VMEM,
+        out_shape=jax.ShapeDtypeStruct((len(pieces), rows, width), jnp.bfloat16),
+        cost_estimate=pl.CostEstimate(
+            flops=rows * width, bytes_accessed=4 * rows * width, transcendentals=0
+        ),
+        compiler_params=pltpu.CompilerParams(vmem_limit_bytes=8 << 20),
+        name="stack",
+    )(*pieces)
+
+
+def respond_kernel(me, band, weights_ref, *rest, planes, per_step, chunk, first, halves, last):
+    rows_in = rest[:planes]
+    cols_in = rest[planes : planes + len(halves)]
+    rest = rest[planes + len(halves) :]
+    acc_ref = None if first else rest[0]
+    out_ref, rows_s, weights_s, scaled_s = rest if first else rest[1:]
+    rows, width = rows_in[0].shape
+    step = pl.program_id(0)
+    side = jnp.bitwise_and(me[0], 1)
+    shift = jnp.bitwise_xor(me[0] // 2, band[0])
+
+    @pl.when(step == 0)
+    def _():
+        for d in range(planes):
+            slot = jnp.bitwise_xor(shift, d)
+            rows_s[slot] = rows_in[d][...]
+            weights_s[slot] = weights_ref[d, :, chunk * width : (chunk + 1) * width]
+
+    for k in range(planes):
+        base = rows_s[k].astype(jnp.float32)
+        for f in range(per_step):
+            w = weights_s[k, pl.ds(step * per_step + f, 1), :]
+            scaled_s[f * rows : (f + 1) * rows, k * width : (k + 1) * width] = (w * base).astype(
+                jnp.bfloat16
+            )
+    here = pl.ds(step * per_step, per_step)
+    for cols, far in zip(cols_in, halves):
+        total = None
+        for k in range(planes):
+            part = lax.dot_general(
+                scaled_s[:, k * width : (k + 1) * width],
+                cols[k],
+                (((1,), (1,)), ((), ())),
+                preferred_element_type=jnp.float32,
+            )
+            total = part if total is None else total + part
+        total = total.reshape(per_step, rows, rows)
+        half = 1 - side if far else side
+        where = pl.ds(pl.multiple_of(half * rows, rows), rows)
+        if acc_ref is not None:
+            total = total + acc_ref[here, :, where]
+        if last:
+            out_ref[:, :, where] = total
+        else:
+            out_ref[here, :, where] = total
+    if last and len(halves) == 1:
+        half = side if halves[0] else 1 - side
+        where = pl.ds(pl.multiple_of(half * rows, rows), rows)
+        out_ref[:, :, where] = acc_ref[here, :, where]
+
+
+def respond(me, band, weights, rows_in, cols_in, halves, acc, chunk, last):
+    planes = len(rows_in)
+    rows, width = rows_in[0].shape
+    nfreq = weights.shape[1]
+    per_step = 4
+    first = acc is None
+    args = [weights, *rows_in, *cols_in]
+    aliases = {}
+    if not first:
+        args.append(acc)
+        if not last:
+            aliases = {len(args) + 1: 0}
+    if last:
+        out_spec = pl.BlockSpec((per_step, rows, 2 * rows), lambda step, me, band: (step, 0, 0))
+    else:
+        out_spec = VMEM
+    return pl.pallas_call(
+        functools.partial(
+            respond_kernel,
+            planes=planes,
+            per_step=per_step,
+            chunk=chunk,
+            first=first,
+            halves=halves,
+            last=last,
+        ),
+        grid_spec=pltpu.PrefetchScalarGridSpec(
+            num_scalar_prefetch=2,
+            grid=(nfreq // per_step,),
+            in_specs=[VMEM] * len(args),
+            out_specs=out_spec,
+            scratch_shapes=[
+                pltpu.VMEM((planes, rows, width), jnp.bfloat16),
+                pltpu.VMEM((planes, nfreq, width), jnp.float32),
+                pltpu.VMEM((per_step * rows, planes * width), jnp.bfloat16),
+            ],
+        ),
+        out_shape=jax.ShapeDtypeStruct((nfreq, rows, 2 * rows), jnp.float32),
+        input_output_aliases=aliases,
+        cost_estimate=pl.CostEstimate(
+            flops=2 * nfreq * rows * rows * len(halves) * planes * width,
+            bytes_accessed=nfreq * rows * 2 * rows * 4,
+            transcendentals=0,
+        ),
+        compiler_params=pltpu.CompilerParams(
+            dimension_semantics=("arbitrary",), vmem_limit_bytes=20 << 20
+        ),
+        name="respond",
+    )(me, band, *args)
+
+
+def grid_on_device(basis_set, densities, pair_gaps, frequencies):
+    planes = lax.axis_size("band")
+    rows = basis_set.shape[1] // lax.axis_size("pw")
+    pairs = densities.shape[1]
+    width = pairs // NBATCH
+    chunks = [NBATCH - 1, *range(NBATCH - 1)]
+
+    def permute(value, move):
+        pairs_of = []
+        for z in range(planes):
+            for x in range(2):
+                for b in range(planes):
+                    tz, tx, tb = move(z, x, b)
+                    pairs_of.append(((z * 2 + x) * planes + b, (tz * 2 + tx) * planes + tb))
+        return lax.ppermute(value, AXES, pairs_of)
+
+    def swap(z, x, b):
+        return (z, 1 - x, b)
+
+    me = lax.axis_index("pw").astype(jnp.int32).reshape(1)
+    band = lax.axis_index("band").astype(jnp.int32).reshape(1)
+
+    def projects(block, count, own):
+        return project(
+            me, basis_set, densities, block, count, width, planes, rows, own
+        )
+
+    away = projects(NBATCH - 1, 1, False) + projects(0, NBATCH - 1, False)
+    kept = projects(NBATCH - 1, 1, True) + projects(0, NBATCH - 1, True)
+    gaps = [pair_gaps.reshape(-1, 128)]
+    for d in range(1, planes):
+        gaps.append(permute(gaps[0], lambda z, x, b, d=d: (z, x, b ^ d)))
+    weights = jnp.stack(
+        [weigh(g.reshape(-1), frequencies, pairs * planes) for g in gaps]
+    )
+
+    acc = None
+    collected = [None] * NBATCH
+    for i, chunk in enumerate(chunks):
+        got = permute(away[i], swap)
+        held, sent = fold(kept[i], got)
+        got = permute(sent, lambda z, x, b: (z ^ 1, x, b))
+        held, sent = fold(held, got)
+        got = permute(sent, lambda z, x, b: (z ^ 2, x, b))
+        (own,) = fold(held, got)
+        collected[chunk] = own
+        near = [permute(own, lambda z, x, b, k=k: (b ^ k, x, z)) for k in range(planes)]
+        rows_in = [own] + [
+            permute(own, lambda z, x, b, d=d: (z, x, b ^ d))
+            for d in range(1, planes)
+        ]
+        near = stack(near)
+        far = permute(near, swap)
+        if i < NBATCH - 1:
+            acc = respond(me, band, weights, rows_in, [near, far], (False, True), acc, chunk, False)
+        else:
+            acc = respond(me, band, weights, rows_in, [near], (False,), acc, chunk, False)
+            acc = respond(me, band, weights, rows_in, [far], (True,), acc, chunk, True)
+    return (acc, jnp.concatenate(collected, axis=1))
+
+
 def solution(mesh):
+    planes = mesh.shape["band"]
+    on_grid = mesh.shape["pw"] == 2 * planes and planes == 4
     in_specs = (P("pw", None), P("pw", "band"), P("band"), P())
     out_specs = (P(None, "pw", "band"), P("pw", "band"))
     return jax.shard_map(
-        on_device, mesh=mesh, in_specs=in_specs, out_specs=out_specs, check_vma=False
+        grid_on_device if on_grid else plain_on_device,
+        mesh=mesh,
+        in_specs=in_specs,
+        out_specs=out_specs,
+        check_vma=False,
     )

time: 569 us -> 181 us (0.32)
  waiting for transfers between devices: 386 us -> 33.5 us
  starting transfers between devices: 15.3 us -> 89.4 us
  matrix products: 72.8 us -> 0 us
  blocking collectives: 55.4 us -> 0 us
  Pallas kernels: 0 us -> 48.8 us
  between operations: 14.3 us -> 1.03 us
  other arithmetic: 12.5 us -> 1 us
    reduce_scatter x4 -> x0, waiting for transfers between devices: 247 us -> none  [on_device(): lax.psum_scatter(lax.dot_general(basis_set, dens_block, (((0,), (0,)), ((...]
    all_gather x4 -> x0, waiting for transfers between devices: 139 us -> none  [on_device(): gathered = lax.all_gather(own_rows, 'pw', axis=0, tiled=True)]
    ppermute x0 -> x47, starting transfers between devices: none -> 89.4 us  [permute(): return lax.ppermute(value, AXES, pairs_of)]
    dot_general x8 -> x0, matrix products: 72.8 us -> none  [the longest x4 40 us: on_device(): lax.dot_general(basis_set, dens_block, (((0,), (0,)), ((), ())), preferre...]
    all_gather x5 -> x0, blocking collectives: 55.4 us -> none  [the longest x4 40 us: on_device(): rows_all = lax.all_gather(own_rows, 'band', axis=1, tiled=True)]
    pallas_call x0 -> x25, Pallas kernels: none -> 48.8 us  [the longest x5 26.3 us: respond(): pl.pallas_call(functools.partial(respond_kernel, planes=planes, per_step=...]
    ppermute x0 -> x47, waiting for transfers between devices: none -> 33.5 us  [permute(): return lax.ppermute(value, AXES, pairs_of)]
    all_to_all x4 -> x0, starting transfers between devices: 14.8 us -> none  [on_device(): lax.all_to_all(gathered, 'band', split_axis=0, concat_axis=1, tiled=True)]
  transfers between devices with their start and end apart: 12 -> 47, of which waited for: 8 -> 7; matrix products, arithmetic and copies ran while one was open for 9% -> 1% of each run, Pallas kernels for 0% -> 22%
where the time goes in v1:
time: 181 us
  starting transfers between devices  89.4 us (49%)
  Pallas kernels  48.8 us (27%)
  waiting for transfers between devices  33.5 us (19%)
  local copies, waits for them, and re-layouts  7.37 us (4%)
    ppermute x47, starting transfers between devices, permute(): return lax.ppermute(value, AXES, pairs_of)  89.4 us
    ppermute x47, waiting for transfers between devices, permute(): return lax.ppermute(value, AXES, pairs_of)  33.5 us
    pallas_call x5, Pallas kernels, respond(): pl.pallas_call(functools.partial(respond_kernel, planes=planes, per_step=...  26.3 us
    pallas_call x4, Pallas kernels, project(): pl.pallas_call(project_kernel, grid_spec=pltpu.PrefetchScalarGridSpec(num...  21.4 us
    unnamed x8, local copies, waits for them, and re-layouts  7.37 us
  transfers between devices with their start and end apart: 47, of which 7 were waited for; matrix products, arithmetic and copies ran while one was open for 1% of the time, Pallas kernels for 22%

profile of v1, /device:TPU:0, one launch (start us, length us, event | category | flops | bytes accessed | tf_op | source)
XLA Modules:
  0.0 181.0 jit_solution(10456970813344629876)
XLA Ops:
  0.6 4.6 %copy-done = bf16[3072,2048]{1,0:T(8,128)(2,1)S(1)} copy-done((bf16[3072,2048]{1,0:T(8,128)(2,1)S(1)}, bf16[3072,2048]{1,0:T(8,128)(2,1)}, u32[]{:S(2)}) %copy-start) | copy-done | bytes 12582936
  5.2 2.8 %copy-done.1 = bf16[3072,1024]{1,0:T(8,128)(2,1)S(1)} copy-done((bf16[3072,1024]{1,0:T(8,128)(2,1)S(1)}, bf16[3072,1024]{1,0:T(8,128)(2,1)}, u32[]{:S(2)}) %copy-start.1) | copy-done | bytes 6291480
  8.0 3.7 %project.7 = bf16[4,256,256]{2,1,0:T(8,128)(2,1)S(1)} custom-call(s32[1]{0:T(128)} %bitcast.me, bf16[3072,1024]{1,0:T(8,128)(2,1)S(1)} %copy-done.1, bf16[3072,2048]{1,0:T(8,128)(2,1)S(1)} %copy-done), custom_call_target="tpu_custom_call" | custom-call | flops 1610612736 | bytes 7864320 | tf_op jit(solution)/shard_map/project/pallas_call | solution.py:78
  11.7 3.0 %collective-permute-start.36 = (bf16[4,256,256]{2,1,0:T(8,128)(2,1)S(1)}, bf16[4,256,256]{2,1,0:T(8,128)(2,1)S(1)}, u32[]{:S(2)}, u32[]{:S(2)}) collective-permute-start(bf16[4,256,256]{2,1,0:T(8,128)(2,1)S(1)} %project.7), channel_id=1, source_target_pairs={{0,4},{1,5},{2,6},{3,7},{4,0},{5,1},{6,2},{7,3},{8,12},{9,13},{10,... | collective-permute-start | bytes 1572872 | tf_op jit(solution)/shard_map/ppermute | solution.py:268
  14.7 7.0 %project.5 = (bf16[4,256,256]{2,1,0:T(8,128)(2,1)S(1)}, bf16[4,256,256]{2,1,0:T(8,128)(2,1)S(1)}, bf16[4,256,256]{2,1,0:T(8,128)(2,1)S(1)}) custom-call(s32[1]{0:T(128)} %bitcast.me, bf16[3072,1024]{1,0:T(8,128)(2,1)S(1)} %copy-done.1, bf16[3072,2048]{1,0:T(8,128)(2,1)S(1)} %copy-done), custom_call_target="tpu_custom_call" | custom-call | flops 4831838208 | bytes 11010048 | tf_op jit(solution)/shard_map/project/pallas_call | solution.py:78
  21.9 2.0 %collective-permute-start.14 = (bf16[4,256,256]{2,1,0:T(8,128)(2,1)S(1)}, bf16[4,256,256]{2,1,0:T(8,128)(2,1)S(1)}, u32[]{:S(2)}, u32[]{:S(2)}) collective-permute-start(bf16[4,256,256]{2,1,0:T(8,128)(2,1)S(1)} %get-tuple-element.31), channel_id=1, source_target_pairs={{0,4},{1,5},{2,6},{3,7},{4,0},{5,1},{6,2},{7,3},{8,12},{9,13},{10,... | collective-permute-start | bytes 1572872 | tf_op jit(solution)/shard_map/ppermute | solution.py:268
  23.9 3.7 %project.6.kept_ref = bf16[4,256,256]{2,1,0:T(8,128)(2,1)S(1)} custom-call(s32[1]{0:T(128)} %bitcast.me, bf16[3072,1024]{1,0:T(8,128)(2,1)S(1)} %copy-done.1, bf16[3072,2048]{1,0:T(8,128)(2,1)S(1)} %copy-done), custom_call_target="tpu_custom_call" | custom-call | flops 1610612736 | bytes 7864320 | tf_op jit(solution)/shard_map/project/pallas_call | solution.py:78
  27.8 2.1 %collective-permute-start.37 = (bf16[2,256,256]{2,1,0:T(8,128)(2,1)S(1)}, bf16[2,256,256]{2,1,0:T(8,128)(2,1)S(1)}, u32[]{:S(2)}, u32[]{:S(2)}) collective-permute-start(bf16[2,256,256]{2,1,0:T(8,128)(2,1)S(1)} %get-tuple-element.43), channel_id=1, source_target_pairs={{0,8},{1,9},{2,10},{3,11},{4,12},{5,13},{6,14},{7,15},{8,0},{9,1},... | collective-permute-start | bytes 786440 | tf_op jit(solution)/shard_map/ppermute | solution.py:268
  29.9 7.0 %project.4 = (bf16[4,256,256]{2,1,0:T(8,128)(2,1)S(1)}, bf16[4,256,256]{2,1,0:T(8,128)(2,1)S(1)}, bf16[4,256,256]{2,1,0:T(8,128)(2,1)S(1)}) custom-call(s32[1]{0:T(128)} %bitcast.me, bf16[3072,1024]{1,0:T(8,128)(2,1)S(1)} %copy-done.1, bf16[3072,2048]{1,0:T(8,128)(2,1)S(1)} %copy-done), custom_call_target="tpu_custom_call" | custom-call | flops 4831838208 | bytes 11010048 | tf_op jit(solution)/shard_map/project/pallas_call | solution.py:78
  36.9 1.8 collective-permute-done.25.got_ref
  38.9 2.2 %collective-permute-start.26 = (bf16[2,256,256]{2,1,0:T(8,128)(2,1)S(1)}, bf16[2,256,256]{2,1,0:T(8,128)(2,1)S(1)}, u32[]{:S(2)}, u32[]{:S(2)}) collective-permute-start(bf16[2,256,256]{2,1,0:T(8,128)(2,1)S(1)} %get-tuple-element.39), channel_id=1, source_target_pairs={{0,8},{1,9},{2,10},{3,11},{4,12},{5,13},{6,14},{7,15},{8,0},{9,1},... | collective-permute-start | bytes 786440 | tf_op jit(solution)/shard_map/ppermute | solution.py:268
  41.0 8.9 %collective-permute-done.14.got_ref = bf16[4,256,256]{2,1,0:T(8,128)(2,1)S(1)} collective-permute-done((bf16[4,256,256]{2,1,0:T(8,128)(2,1)S(1)}, bf16[4,256,256]{2,1,0:T(8,128)(2,1)S(1)}, u32[]{:S(2)}, u32[]{:S(2)}) %collective-permute-start.14) | collective-permute-done | bytes 524320 | tf_op jit(solution)/shard_map/ppermute | solution.py:268
  50.1 2.2 %collective-permute-start.15 = (bf16[2,256,256]{2,1,0:T(8,128)(2,1)S(1)}, bf16[2,256,256]{2,1,0:T(8,128)(2,1)S(1)}, u32[]{:S(2)}, u32[]{:S(2)}) collective-permute-start(bf16[2,256,256]{2,1,0:T(8,128)(2,1)S(1)} %get-tuple-element.33), channel_id=1, source_target_pairs={{0,8},{1,9},{2,10},{3,11},{4,12},{5,13},{6,14},{7,15},{8,0},{9,1},... | collective-permute-start | bytes 786440 | tf_op jit(solution)/shard_map/ppermute | solution.py:268
  52.3 2.7 %collective-permute-start.38 = (bf16[1,256,256]{2,1,0:T(8,128)(2,1)S(1)}, bf16[1,256,256]{2,1,0:T(8,128)(2,1)S(1)}, u32[]{:S(2)}, u32[]{:S(2)}) collective-permute-start(bf16[1,256,256]{2,1,0:T(8,128)(2,1)S(1)} %get-tuple-element.45), channel_id=1, source_target_pairs={{0,16},{1,17},{2,18},{3,19},{4,20},{5,21},{6,22},{7,23},{8,24},{9,... | collective-permute-start | bytes 393224 | tf_op jit(solution)/shard_map/ppermute | solution.py:268
  55.0 5.4 %collective-permute-done.3.got_ref = bf16[4,256,256]{2,1,0:T(8,128)(2,1)S(1)} collective-permute-done((bf16[4,256,256]{2,1,0:T(8,128)(2,1)S(1)}, bf16[4,256,256]{2,1,0:T(8,128)(2,1)S(1)}, u32[]{:S(2)}, u32[]{:S(2)}) %collective-permute-start.3) | collective-permute-done | bytes 524320 | tf_op jit(solution)/shard_map/ppermute | solution.py:268
  60.5 1.9 %collective-permute-start.4 = (bf16[2,256,256]{2,1,0:T(8,128)(2,1)S(1)}, bf16[2,256,256]{2,1,0:T(8,128)(2,1)S(1)}, u32[]{:S(2)}, u32[]{:S(2)}) collective-permute-start(bf16[2,256,256]{2,1,0:T(8,128)(2,1)S(1)} %get-tuple-element.27), channel_id=1, source_target_pairs={{0,8},{1,9},{2,10},{3,11},{4,12},{5,13},{6,14},{7,15},{8,0},{9,1},... | collective-permute-start | bytes 786440 | tf_op jit(solution)/shard_map/ppermute | solution.py:268
  62.4 1.6 collective-permute-start.1
  64.4 2.6 %collective-permute-start.27 = (bf16[1,256,256]{2,1,0:T(8,128)(2,1)S(1)}, bf16[1,256,256]{2,1,0:T(8,128)(2,1)S(1)}, u32[]{:S(2)}, u32[]{:S(2)}) collective-permute-start(bf16[1,256,256]{2,1,0:T(8,128)(2,1)S(1)} %get-tuple-element.41), channel_id=1, source_target_pairs={{0,16},{1,17},{2,18},{3,19},{4,20},{5,21},{6,22},{7,23},{8,24},{9,... | collective-permute-start | bytes 393224 | tf_op jit(solution)/shard_map/ppermute | solution.py:268
  68.2 2.7 %collective-permute-start.43 = (bf16[256,256]{1,0:T(8,128)(2,1)S(1)}, bf16[256,256]{1,0:T(8,128)(2,1)S(1)}, u32[]{:S(2)}, u32[]{:S(2)}) collective-permute-start(bf16[256,256]{1,0:T(8,128)(2,1)S(1)} %fold.23.rest_0_), channel_id=1, source_target_pairs={{0,8},{1,0},{2,24},{3,16},{4,12},{5,4},{6,28},{7,20},{8,9},{9,1},{... | collective-permute-start | bytes 393224 | tf_op jit(solution)/shard_map/ppermute | solution.py:268
  70.9 3.5 %collective-permute-start.44 = (bf16[256,256]{1,0:T(8,128)(2,1)S(1)}, bf16[256,256]{1,0:T(8,128)(2,1)S(1)}, u32[]{:S(2)}, u32[]{:S(2)}) collective-permute-start(bf16[256,256]{1,0:T(8,128)(2,1)S(1)} %fold.23.rest_0_), channel_id=1, source_target_pairs={{0,16},{1,24},{2,0},{3,8},{4,20},{5,28},{6,4},{7,12},{8,17},{9,25}... | collective-permute-start | bytes 393224 | tf_op jit(solution)/shard_map/ppermute | solution.py:268
  74.4 8.1 %collective-permute-done.27.got_ref = bf16[1,256,256]{2,1,0:T(8,128)(2,1)S(1)} collective-permute-done((bf16[1,256,256]{2,1,0:T(8,128)(2,1)S(1)}, bf16[1,256,256]{2,1,0:T(8,128)(2,1)S(1)}, u32[]{:S(2)}, u32[]{:S(2)}) %collective-permute-start.27) | collective-permute-done | bytes 131104 | tf_op jit(solution)/shard_map/ppermute | solution.py:268
  82.6 4.1 %collective-permute-done.16.got_ref = bf16[1,256,256]{2,1,0:T(8,128)(2,1)S(1)} collective-permute-done((bf16[1,256,256]{2,1,0:T(8,128)(2,1)S(1)}, bf16[1,256,256]{2,1,0:T(8,128)(2,1)S(1)}, u32[]{:S(2)}, u32[]{:S(2)}) %collective-permute-start.16) | collective-permute-done | bytes 131104 | tf_op jit(solution)/shard_map/ppermute | solution.py:268
  88.4 11.2 %collective-permute-start.33 = (bf16[256,256]{1,0:T(8,128)(2,1)S(1)}, bf16[256,256]{1,0:T(8,128)(2,1)S(1)}, u32[]{:S(2)}, u32[]{:S(2)}) collective-permute-start(bf16[256,256]{1,0:T(8,128)(2,1)S(1)} %fold.20.rest_0_), channel_id=1, source_target_pairs={{0,16},{1,24},{2,0},{3,8},{4,20},{5,28},{6,4},{7,12},{8,17},{9,25}... | collective-permute-start | bytes 393224 | tf_op jit(solution)/shard_map/ppermute | solution.py:268
  100.8 3.0 %collective-permute-start.21 = (bf16[256,256]{1,0:T(8,128)(2,1)S(1)}, bf16[256,256]{1,0:T(8,128)(2,1)S(1)}, u32[]{:S(2)}, u32[]{:S(2)}) collective-permute-start(bf16[256,256]{1,0:T(8,128)(2,1)S(1)} %fold.17.rest_0_), channel_id=1, source_target_pairs={{0,8},{1,0},{2,24},{3,16},{4,12},{5,4},{6,28},{7,20},{8,9},{9,1},{... | collective-permute-start | bytes 393224 | tf_op jit(solution)/shard_map/ppermute | solution.py:268
  103.8 5.1 %collective-permute-start.22 = (bf16[256,256]{1,0:T(8,128)(2,1)S(1)}, bf16[256,256]{1,0:T(8,128)(2,1)S(1)}, u32[]{:S(2)}, u32[]{:S(2)}) collective-permute-start(bf16[256,256]{1,0:T(8,128)(2,1)S(1)} %fold.17.rest_0_), channel_id=1, source_target_pairs={{0,16},{1,24},{2,0},{3,8},{4,20},{5,28},{6,4},{7,12},{8,17},{9,25}... | collective-permute-start | bytes 393224 | tf_op jit(solution)/shard_map/ppermute | solution.py:268
  108.8 1.1 collective-permute-start.23
  109.9 1.5 collective-permute-start.46
  111.5 7.8 %collective-permute-start.10 = (bf16[256,256]{1,0:T(8,128)(2,1)S(1)}, bf16[256,256]{1,0:T(8,128)(2,1)S(1)}, u32[]{:S(2)}, u32[]{:S(2)}) collective-permute-start(bf16[256,256]{1,0:T(8,128)(2,1)S(1)} %fold.14.rest_0_), channel_id=1, source_target_pairs={{0,8},{1,0},{2,24},{3,16},{4,12},{5,4},{6,28},{7,20},{8,9},{9,1},{... | collective-permute-start | bytes 393224 | tf_op jit(solution)/shard_map/ppermute | solution.py:268
  119.3 2.6 %collective-permute-start.11 = (bf16[256,256]{1,0:T(8,128)(2,1)S(1)}, bf16[256,256]{1,0:T(8,128)(2,1)S(1)}, u32[]{:S(2)}, u32[]{:S(2)}) collective-permute-start(bf16[256,256]{1,0:T(8,128)(2,1)S(1)} %fold.14.rest_0_), channel_id=1, source_target_pairs={{0,16},{1,24},{2,0},{3,8},{4,20},{5,28},{6,4},{7,12},{8,17},{9,25}... | collective-permute-start | bytes 393224 | tf_op jit(solution)/shard_map/ppermute | solution.py:268
  121.9 0.8 collective-permute-start.9
  122.9 4.4 %collective-permute-start.39 = (bf16[256,256]{1,0:T(8,128)(2,1)S(1)}, bf16[256,256]{1,0:T(8,128)(2,1)S(1)}, u32[]{:S(2)}, u32[]{:S(2)}) collective-permute-start(bf16[256,256]{1,0:T(8,128)(2,1)S(1)} %fold.23.rest_0_), channel_id=1, source_target_pairs={{0,1},{1,0},{2,3},{3,2},{4,5},{5,4},{6,7},{7,6},{8,9},{9,8},{10,11... | collective-permute-start | bytes 393224 | tf_op jit(solution)/shard_map/ppermute | solution.py:268
  127.3 7.4 %collective-permute-start.40 = (bf16[256,256]{1,0:T(8,128)(2,1)S(1)}, bf16[256,256]{1,0:T(8,128)(2,1)S(1)}, u32[]{:S(2)}, u32[]{:S(2)}) collective-permute-start(bf16[256,256]{1,0:T(8,128)(2,1)S(1)} %fold.23.rest_0_), channel_id=1, source_target_pairs={{0,2},{1,3},{2,0},{3,1},{4,6},{5,7},{6,4},{7,5},{8,10},{9,11},{10,... | collective-permute-start | bytes 393224 | tf_op jit(solution)/shard_map/ppermute | solution.py:268
  134.8 1.6 collective-permute-start.35
  136.4 0.9 pad_maximum_fusion
  137.4 1.7 collective-permute-start.28
  139.0 0.9 collective-permute-done.40.rest_2_
  140.0 3.7 %collective-permute-start.29 = (bf16[256,256]{1,0:T(8,128)(2,1)S(1)}, bf16[256,256]{1,0:T(8,128)(2,1)S(1)}, u32[]{:S(2)}, u32[]{:S(2)}) collective-permute-start(bf16[256,256]{1,0:T(8,128)(2,1)S(1)} %fold.20.rest_0_), channel_id=1, source_target_pairs={{0,2},{1,3},{2,0},{3,1},{4,6},{5,7},{6,4},{7,5},{8,10},{9,11},{10,... | collective-permute-start | bytes 393224 | tf_op jit(solution)/shard_map/ppermute | solution.py:268
  143.6 0.8 collective-permute-start.30
  144.4 1.5 collective-permute-start.24
  145.9 5.5 %respond.5.rest_6_ = f32[16,256,512]{2,1,0:T(8,128)S(1)} custom-call(s32[1]{0:T(128)} %bitcast.me, s32[1]{0:T(128)} %bitcast.1.band, f32[4,16,1024]{2,1,0:T(8,128)S(1)} %pad_maximum_fusion.1.weights_ref, bf16[256,256]{1,0:T(8,128)(2,1)S(1)} %fold.23.rest_0_, bf16[256,256]{1,0:T(8,128)(2,1)S(1)} %collective-permute-done.39.rest_1_, ...), custom_call_target="tpu_custom_call" | custom-call | flops 4294967296 | bytes 8388608 | tf_op jit(solution)/shard_map/respond/pallas_call | solution.py:219
  151.7 1.7 collective-permute-start.19
  153.8 6.2 %respond.6.rest_6_ = f32[16,256,512]{2,1,0:T(8,128)S(1)} custom-call(s32[1]{0:T(128)} %bitcast.me, s32[1]{0:T(128)} %bitcast.1.band, f32[4,16,1024]{2,1,0:T(8,128)S(1)} %pad_maximum_fusion.1.weights_ref, bf16[256,256]{1,0:T(8,128)(2,1)S(1)} %fold.20.rest_0_, bf16[256,256]{1,0:T(8,128)(2,1)S(1)} %collective-permute-done.28.rest_1_, ...), custom_call_target="tpu_custom_call", output_to_operand_aliasing={{}: (9, {})} | custom-call | flops 4294967296 | bytes 8388608 | tf_op jit(solution)/shard_map/respond/pallas_call | solution.py:219
  160.1 1.4 collective-permute-start.8
  161.5 0.7 collective-permute-start.13
  162.2 6.2 %respond.7.rest_5_ = f32[16,256,512]{2,1,0:T(8,128)S(1)} custom-call(s32[1]{0:T(128)} %bitcast.me, s32[1]{0:T(128)} %bitcast.1.band, f32[4,16,1024]{2,1,0:T(8,128)S(1)} %pad_maximum_fusion.1.weights_ref, bf16[256,256]{1,0:T(8,128)(2,1)S(1)} %fold.17.rest_0_, bf16[256,256]{1,0:T(8,128)(2,1)S(1)} %collective-permute-done.17.rest_1_, ...), custom_call_target="tpu_custom_call", output_to_operand_aliasing={{}: (9, {})} | custom-call | flops 4294967296 | bytes 8388608 | tf_op jit(solution)/shard_map/respond/pallas_call | solution.py:219
  168.5 3.4 %respond.8.rest_5_ = f32[16,256,512]{2,1,0:T(8,128)S(1)} custom-call(s32[1]{0:T(128)} %bitcast.me, s32[1]{0:T(128)} %bitcast.1.band, f32[4,16,1024]{2,1,0:T(8,128)S(1)} %pad_maximum_fusion.1.weights_ref, bf16[256,256]{1,0:T(8,128)(2,1)S(1)} %fold.14.rest_0_, bf16[256,256]{1,0:T(8,128)(2,1)S(1)} %collective-permute-done.6.rest_1_, ...), custom_call_target="tpu_custom_call", output_to_operand_aliasing={{}: (8, {})} | custom-call | flops 2147483648 | bytes 8388608 | tf_op jit(solution)/shard_map/respond/pallas_call | solution.py:219
  171.9 4.1 %collective-permute-done.13.rest_4_ = bf16[4,256,256]{2,1,0:T(8,128)(2,1)S(1)} collective-permute-done((bf16[4,256,256]{2,1,0:T(8,128)(2,1)S(1)}, bf16[4,256,256]{2,1,0:T(8,128)(2,1)S(1)}, u32[]{:S(2)}, u32[]{:S(2)}) %collective-permute-start.13) | collective-permute-done | bytes 524320 | tf_op jit(solution)/shard_map/ppermute | solution.py:268
  176.0 5.0 %respond.9 = f32[16,256,512]{2,1,0:T(8,128)} custom-call(s32[1]{0:T(128)} %bitcast.me, s32[1]{0:T(128)} %bitcast.1.band, f32[4,16,1024]{2,1,0:T(8,128)S(1)} %pad_maximum_fusion.1.weights_ref, bf16[256,256]{1,0:T(8,128)(2,1)S(1)} %fold.14.rest_0_, bf16[256,256]{1,0:T(8,128)(2,1)S(1)} %collective-permute-done.6.rest_1_, ...), custom_call_target="tpu_custom_call" | custom-call | flops 2147483648 | bytes 8388608 | tf_op jit(solution)/shard_map/respond/pallas_call | solution.py:219
  (87 shorter events, 6.4 us)
Async XLA Ops:
  11.7 15.9 %collective-permute-start.36 = (bf16[4,256,256]{2,1,0:T(8,128)(2,1)S(1)}, bf16[4,256,256]{2,1,0:T(8,128)(2,1)S(1)}, u32[]{:S(2)}, u32[]{:S(2)}) collective-permute-start(bf16[4,256,256]{2,1,0:T(8,128)(2,1)S(1)} %project.7), channel_id=1, source_target_pairs={{0,4},{1,5},{2,6},{3,7},{4,0},{5,1},{6,2},{7,3},{8,12},{9,13},{10,... | collective-permute-start | bytes 1572872 | tf_op jit(solution)/shard_map/ppermute | solution.py:268
  21.8 17.0 %collective-permute-start.25 = (bf16[4,256,256]{2,1,0:T(8,128)(2,1)S(1)}, bf16[4,256,256]{2,1,0:T(8,128)(2,1)S(1)}, u32[]{:S(2)}, u32[]{:S(2)}) collective-permute-start(bf16[4,256,256]{2,1,0:T(8,128)(2,1)S(1)} %get-tuple-element.37), channel_id=1, source_target_pairs={{0,4},{1,5},{2,6},{3,7},{4,0},{5,1},{6,2},{7,3},{8,12},{9,13},{10,... | collective-permute-start | bytes 1572872 | tf_op jit(solution)/shard_map/ppermute | solution.py:268
  21.9 28.1 %collective-permute-start.14 = (bf16[4,256,256]{2,1,0:T(8,128)(2,1)S(1)}, bf16[4,256,256]{2,1,0:T(8,128)(2,1)S(1)}, u32[]{:S(2)}, u32[]{:S(2)}) collective-permute-start(bf16[4,256,256]{2,1,0:T(8,128)(2,1)S(1)} %get-tuple-element.31), channel_id=1, source_target_pairs={{0,4},{1,5},{2,6},{3,7},{4,0},{5,1},{6,2},{7,3},{8,12},{9,13},{10,... | collective-permute-start | bytes 1572872 | tf_op jit(solution)/shard_map/ppermute | solution.py:268
  23.9 36.5 %collective-permute-start.3 = (bf16[4,256,256]{2,1,0:T(8,128)(2,1)S(1)}, bf16[4,256,256]{2,1,0:T(8,128)(2,1)S(1)}, u32[]{:S(2)}, u32[]{:S(2)}) collective-permute-start(bf16[4,256,256]{2,1,0:T(8,128)(2,1)S(1)} %get-tuple-element.25), channel_id=1, source_target_pairs={{0,4},{1,5},{2,6},{3,7},{4,0},{5,1},{6,2},{7,3},{8,12},{9,13},{10,... | collective-permute-start | bytes 1572872 | tf_op jit(solution)/shard_map/ppermute | solution.py:268
  27.8 39.2 %copy-start.3 = (f32[16]{0:T(128)S(1)}, f32[16]{0:T(128)}, u32[]{:S(2)}) copy-start(f32[16]{0:T(128)} %param.7) | copy-start | bytes 196
  27.8 24.5 %collective-permute-start.37 = (bf16[2,256,256]{2,1,0:T(8,128)(2,1)S(1)}, bf16[2,256,256]{2,1,0:T(8,128)(2,1)S(1)}, u32[]{:S(2)}, u32[]{:S(2)}) collective-permute-start(bf16[2,256,256]{2,1,0:T(8,128)(2,1)S(1)} %get-tuple-element.43), channel_id=1, source_target_pairs={{0,8},{1,9},{2,10},{3,11},{4,12},{5,13},{6,14},{7,15},{8,0},{9,1},... | collective-permute-start | bytes 786440 | tf_op jit(solution)/shard_map/ppermute | solution.py:268
  38.9 23.5 %collective-permute-start.26 = (bf16[2,256,256]{2,1,0:T(8,128)(2,1)S(1)}, bf16[2,256,256]{2,1,0:T(8,128)(2,1)S(1)}, u32[]{:S(2)}, u32[]{:S(2)}) collective-permute-start(bf16[2,256,256]{2,1,0:T(8,128)(2,1)S(1)} %get-tuple-element.39), channel_id=1, source_target_pairs={{0,8},{1,9},{2,10},{3,11},{4,12},{5,13},{6,14},{7,15},{8,0},{9,1},... | collective-permute-start | bytes 786440 | tf_op jit(solution)/shard_map/ppermute | solution.py:268
  50.1 13.9 %collective-permute-start.15 = (bf16[2,256,256]{2,1,0:T(8,128)(2,1)S(1)}, bf16[2,256,256]{2,1,0:T(8,128)(2,1)S(1)}, u32[]{:S(2)}, u32[]{:S(2)}) collective-permute-start(bf16[2,256,256]{2,1,0:T(8,128)(2,1)S(1)} %get-tuple-element.33), channel_id=1, source_target_pairs={{0,8},{1,9},{2,10},{3,11},{4,12},{5,13},{6,14},{7,15},{8,0},{9,1},... | collective-permute-start | bytes 786440 | tf_op jit(solution)/shard_map/ppermute | solution.py:268
  52.3 12.0 %collective-permute-start.38 = (bf16[1,256,256]{2,1,0:T(8,128)(2,1)S(1)}, bf16[1,256,256]{2,1,0:T(8,128)(2,1)S(1)}, u32[]{:S(2)}, u32[]{:S(2)}) collective-permute-start(bf16[1,256,256]{2,1,0:T(8,128)(2,1)S(1)} %get-tuple-element.45), channel_id=1, source_target_pairs={{0,16},{1,17},{2,18},{3,19},{4,20},{5,21},{6,22},{7,23},{8,24},{9,... | collective-permute-start | bytes 393224 | tf_op jit(solution)/shard_map/ppermute | solution.py:268
  60.5 10.4 %collective-permute-start.4 = (bf16[2,256,256]{2,1,0:T(8,128)(2,1)S(1)}, bf16[2,256,256]{2,1,0:T(8,128)(2,1)S(1)}, u32[]{:S(2)}, u32[]{:S(2)}) collective-permute-start(bf16[2,256,256]{2,1,0:T(8,128)(2,1)S(1)} %get-tuple-element.27), channel_id=1, source_target_pairs={{0,8},{1,9},{2,10},{3,11},{4,12},{5,13},{6,14},{7,15},{8,0},{9,1},... | collective-permute-start | bytes 786440 | tf_op jit(solution)/shard_map/ppermute | solution.py:268
  62.4 4.7 %collective-permute-start = (f32[8,128]{1,0:T(8,128)S(1)}, f32[8,128]{1,0:T(8,128)S(1)}, u32[]{:S(2)}, u32[]{:S(2)}) collective-permute-start(f32[8,128]{1,0:T(8,128)S(1)} %bitcast.15), channel_id=1, source_target_pairs={{0,1},{1,0},{2,3},{3,2},{4,5},{5,4},{6,7},{7,6},{8,9},{9,8},{10,11... | collective-permute-start | bytes 12296 | tf_op jit(solution)/shard_map/ppermute | solution.py:268
  62.4 5.1 %collective-permute-start.1 = (f32[8,128]{1,0:T(8,128)S(1)}, f32[8,128]{1,0:T(8,128)S(1)}, u32[]{:S(2)}, u32[]{:S(2)}) collective-permute-start(f32[8,128]{1,0:T(8,128)S(1)} %bitcast.16), channel_id=1, source_target_pairs={{0,2},{1,3},{2,0},{3,1},{4,6},{5,7},{6,4},{7,5},{8,10},{9,11},{10,... | collective-permute-start | bytes 12296 | tf_op jit(solution)/shard_map/ppermute | solution.py:268
  64.0 4.1 %collective-permute-start.2 = (f32[8,128]{1,0:T(8,128)S(1)}, f32[8,128]{1,0:T(8,128)S(1)}, u32[]{:S(2)}, u32[]{:S(2)}) collective-permute-start(f32[8,128]{1,0:T(8,128)S(1)} %bitcast.17), channel_id=1, source_target_pairs={{0,3},{1,2},{2,1},{3,0},{4,7},{5,6},{6,5},{7,4},{8,11},{9,10},{10,... | collective-permute-start | bytes 12296 | tf_op jit(solution)/shard_map/ppermute | solution.py:268
  64.4 18.1 %collective-permute-start.27 = (bf16[1,256,256]{2,1,0:T(8,128)(2,1)S(1)}, bf16[1,256,256]{2,1,0:T(8,128)(2,1)S(1)}, u32[]{:S(2)}, u32[]{:S(2)}) collective-permute-start(bf16[1,256,256]{2,1,0:T(8,128)(2,1)S(1)} %get-tuple-element.41), channel_id=1, source_target_pairs={{0,16},{1,17},{2,18},{3,19},{4,20},{5,21},{6,22},{7,23},{8,24},{9,... | collective-permute-start | bytes 393224 | tf_op jit(solution)/shard_map/ppermute | solution.py:268
  67.1 19.6 %collective-permute-start.16 = (bf16[1,256,256]{2,1,0:T(8,128)(2,1)S(1)}, bf16[1,256,256]{2,1,0:T(8,128)(2,1)S(1)}, u32[]{:S(2)}, u32[]{:S(2)}) collective-permute-start(bf16[1,256,256]{2,1,0:T(8,128)(2,1)S(1)} %get-tuple-element.35), channel_id=1, source_target_pairs={{0,16},{1,17},{2,18},{3,19},{4,20},{5,21},{6,22},{7,23},{8,24},{9,... | collective-permute-start | bytes 393224 | tf_op jit(solution)/shard_map/ppermute | solution.py:268
  67.5 19.6 %collective-permute-start.42 = (bf16[256,256]{1,0:T(8,128)(2,1)S(1)}, bf16[256,256]{1,0:T(8,128)(2,1)S(1)}, u32[]{:S(2)}, u32[]{:S(2)}) collective-permute-start(bf16[256,256]{1,0:T(8,128)(2,1)S(1)} %fold.23.rest_0_), channel_id=1, source_target_pairs={{0,0},{1,8},{2,16},{3,24},{4,4},{5,12},{6,20},{7,28},{8,1},{9,9},{... | collective-permute-start | bytes 393224 | tf_op jit(solution)/shard_map/ppermute | solution.py:268
  68.2 19.6 %collective-permute-start.43 = (bf16[256,256]{1,0:T(8,128)(2,1)S(1)}, bf16[256,256]{1,0:T(8,128)(2,1)S(1)}, u32[]{:S(2)}, u32[]{:S(2)}) collective-permute-start(bf16[256,256]{1,0:T(8,128)(2,1)S(1)} %fold.23.rest_0_), channel_id=1, source_target_pairs={{0,8},{1,0},{2,24},{3,16},{4,12},{5,4},{6,28},{7,20},{8,9},{9,1},{... | collective-permute-start | bytes 393224 | tf_op jit(solution)/shard_map/ppermute | solution.py:268
  70.9 17.5 %collective-permute-start.44 = (bf16[256,256]{1,0:T(8,128)(2,1)S(1)}, bf16[256,256]{1,0:T(8,128)(2,1)S(1)}, u32[]{:S(2)}, u32[]{:S(2)}) collective-permute-start(bf16[256,256]{1,0:T(8,128)(2,1)S(1)} %fold.23.rest_0_), channel_id=1, source_target_pairs={{0,16},{1,24},{2,0},{3,8},{4,20},{5,28},{6,4},{7,12},{8,17},{9,25}... | collective-permute-start | bytes 393224 | tf_op jit(solution)/shard_map/ppermute | solution.py:268
  82.5 17.1 %collective-permute-start.45 = (bf16[256,256]{1,0:T(8,128)(2,1)S(1)}, bf16[256,256]{1,0:T(8,128)(2,1)S(1)}, u32[]{:S(2)}, u32[]{:S(2)}) collective-permute-start(bf16[256,256]{1,0:T(8,128)(2,1)S(1)} %fold.23.rest_0_), channel_id=1, source_target_pairs={{0,24},{1,16},{2,8},{3,0},{4,28},{5,20},{6,12},{7,4},{8,25},{9,17}... | collective-permute-start | bytes 393224 | tf_op jit(solution)/shard_map/ppermute | solution.py:268
  86.7 13.4 %collective-permute-start.5 = (bf16[1,256,256]{2,1,0:T(8,128)(2,1)S(1)}, bf16[1,256,256]{2,1,0:T(8,128)(2,1)S(1)}, u32[]{:S(2)}, u32[]{:S(2)}) collective-permute-start(bf16[1,256,256]{2,1,0:T(8,128)(2,1)S(1)} %get-tuple-element.29), channel_id=1, source_target_pairs={{0,16},{1,17},{2,18},{3,19},{4,20},{5,21},{6,22},{7,23},{8,24},{9,... | collective-permute-start | bytes 393224 | tf_op jit(solution)/shard_map/ppermute | solution.py:268
  87.1 13.6 %collective-permute-start.31 = (bf16[256,256]{1,0:T(8,128)(2,1)S(1)}, bf16[256,256]{1,0:T(8,128)(2,1)S(1)}, u32[]{:S(2)}, u32[]{:S(2)}) collective-permute-start(bf16[256,256]{1,0:T(8,128)(2,1)S(1)} %fold.20.rest_0_), channel_id=1, source_target_pairs={{0,0},{1,8},{2,16},{3,24},{4,4},{5,12},{6,20},{7,28},{8,1},{9,9},{... | collective-permute-start | bytes 393224 | tf_op jit(solution)/shard_map/ppermute | solution.py:268
  87.8 16.0 %collective-permute-start.32 = (bf16[256,256]{1,0:T(8,128)(2,1)S(1)}, bf16[256,256]{1,0:T(8,128)(2,1)S(1)}, u32[]{:S(2)}, u32[]{:S(2)}) collective-permute-start(bf16[256,256]{1,0:T(8,128)(2,1)S(1)} %fold.20.rest_0_), channel_id=1, source_target_pairs={{0,8},{1,0},{2,24},{3,16},{4,12},{5,4},{6,28},{7,20},{8,9},{9,1},{... | collective-permute-start | bytes 393224 | tf_op jit(solution)/shard_map/ppermute | solution.py:268
  88.4 20.4 %collective-permute-start.33 = (bf16[256,256]{1,0:T(8,128)(2,1)S(1)}, bf16[256,256]{1,0:T(8,128)(2,1)S(1)}, u32[]{:S(2)}, u32[]{:S(2)}) collective-permute-start(bf16[256,256]{1,0:T(8,128)(2,1)S(1)} %fold.20.rest_0_), channel_id=1, source_target_pairs={{0,16},{1,24},{2,0},{3,8},{4,20},{5,28},{6,4},{7,12},{8,17},{9,25}... | collective-permute-start | bytes 393224 | tf_op jit(solution)/shard_map/ppermute | solution.py:268
  99.6 10.3 %collective-permute-start.34 = (bf16[256,256]{1,0:T(8,128)(2,1)S(1)}, bf16[256,256]{1,0:T(8,128)(2,1)S(1)}, u32[]{:S(2)}, u32[]{:S(2)}) collective-permute-start(bf16[256,256]{1,0:T(8,128)(2,1)S(1)} %fold.20.rest_0_), channel_id=1, source_target_pairs={{0,24},{1,16},{2,8},{3,0},{4,28},{5,20},{6,12},{7,4},{8,25},{9,17}... | collective-permute-start | bytes 393224 | tf_op jit(solution)/shard_map/ppermute | solution.py:268
  100.1 11.4 %collective-permute-start.20 = (bf16[256,256]{1,0:T(8,128)(2,1)S(1)}, bf16[256,256]{1,0:T(8,128)(2,1)S(1)}, u32[]{:S(2)}, u32[]{:S(2)}) collective-permute-start(bf16[256,256]{1,0:T(8,128)(2,1)S(1)} %fold.17.rest_0_), channel_id=1, source_target_pairs={{0,0},{1,8},{2,16},{3,24},{4,4},{5,12},{6,20},{7,28},{8,1},{9,9},{... | collective-permute-start | bytes 393224 | tf_op jit(solution)/shard_map/ppermute | solution.py:268
  100.8 18.5 %collective-permute-start.21 = (bf16[256,256]{1,0:T(8,128)(2,1)S(1)}, bf16[256,256]{1,0:T(8,128)(2,1)S(1)}, u32[]{:S(2)}, u32[]{:S(2)}) collective-permute-start(bf16[256,256]{1,0:T(8,128)(2,1)S(1)} %fold.17.rest_0_), channel_id=1, source_target_pairs={{0,8},{1,0},{2,24},{3,16},{4,12},{5,4},{6,28},{7,20},{8,9},{9,1},{... | collective-permute-start | bytes 393224 | tf_op jit(solution)/shard_map/ppermute | solution.py:268
  103.8 18.1 %collective-permute-start.22 = (bf16[256,256]{1,0:T(8,128)(2,1)S(1)}, bf16[256,256]{1,0:T(8,128)(2,1)S(1)}, u32[]{:S(2)}, u32[]{:S(2)}) collective-permute-start(bf16[256,256]{1,0:T(8,128)(2,1)S(1)} %fold.17.rest_0_), channel_id=1, source_target_pairs={{0,16},{1,24},{2,0},{3,8},{4,20},{5,28},{6,4},{7,12},{8,17},{9,25}... | collective-permute-start | bytes 393224 | tf_op jit(solution)/shard_map/ppermute | solution.py:268
  108.8 13.1 %collective-permute-start.23 = (bf16[256,256]{1,0:T(8,128)(2,1)S(1)}, bf16[256,256]{1,0:T(8,128)(2,1)S(1)}, u32[]{:S(2)}, u32[]{:S(2)}) collective-permute-start(bf16[256,256]{1,0:T(8,128)(2,1)S(1)} %fold.17.rest_0_), channel_id=1, source_target_pairs={{0,24},{1,16},{2,8},{3,0},{4,28},{5,20},{6,12},{7,4},{8,25},{9,17}... | collective-permute-start | bytes 393224 | tf_op jit(solution)/shard_map/ppermute | solution.py:268
  109.9 34.5 %collective-permute-start.46 = (bf16[4,256,256]{2,1,0:T(8,128)(2,1)S(1)}, bf16[4,256,256]{2,1,0:T(8,128)(2,1)S(1)}, u32[]{:S(2)}, u32[]{:S(2)}) collective-permute-start(bf16[4,256,256]{2,1,0:T(8,128)(2,1)S(1)} %stack.15.rest_4_), channel_id=1, source_target_pairs={{0,4},{1,5},{2,6},{3,7},{4,0},{5,1},{6,2},{7,3},{8,12},{9,13},{10,... | collective-permute-start | bytes 1572872 | tf_op jit(solution)/shard_map/ppermute | solution.py:268
  111.5 11.4 %collective-permute-start.10 = (bf16[256,256]{1,0:T(8,128)(2,1)S(1)}, bf16[256,256]{1,0:T(8,128)(2,1)S(1)}, u32[]{:S(2)}, u32[]{:S(2)}) collective-permute-start(bf16[256,256]{1,0:T(8,128)(2,1)S(1)} %fold.14.rest_0_), channel_id=1, source_target_pairs={{0,8},{1,0},{2,24},{3,16},{4,12},{5,4},{6,28},{7,20},{8,9},{9,1},{... | collective-permute-start | bytes 393224 | tf_op jit(solution)/shard_map/ppermute | solution.py:268
  119.3 8.0 %collective-permute-start.11 = (bf16[256,256]{1,0:T(8,128)(2,1)S(1)}, bf16[256,256]{1,0:T(8,128)(2,1)S(1)}, u32[]{:S(2)}, u32[]{:S(2)}) collective-permute-start(bf16[256,256]{1,0:T(8,128)(2,1)S(1)} %fold.14.rest_0_), channel_id=1, source_target_pairs={{0,16},{1,24},{2,0},{3,8},{4,20},{5,28},{6,4},{7,12},{8,17},{9,25}... | collective-permute-start | bytes 393224 | tf_op jit(solution)/shard_map/ppermute | solution.py:268
  121.9 12.8 %collective-permute-start.12 = (bf16[256,256]{1,0:T(8,128)(2,1)S(1)}, bf16[256,256]{1,0:T(8,128)(2,1)S(1)}, u32[]{:S(2)}, u32[]{:S(2)}) collective-permute-start(bf16[256,256]{1,0:T(8,128)(2,1)S(1)} %fold.14.rest_0_), channel_id=1, source_target_pairs={{0,24},{1,16},{2,8},{3,0},{4,28},{5,20},{6,12},{7,4},{8,25},{9,17}... | collective-permute-start | bytes 393224 | tf_op jit(solution)/shard_map/ppermute | solution.py:268
  121.9 12.9 %collective-permute-start.9 = (bf16[256,256]{1,0:T(8,128)(2,1)S(1)}, bf16[256,256]{1,0:T(8,128)(2,1)S(1)}, u32[]{:S(2)}, u32[]{:S(2)}) collective-permute-start(bf16[256,256]{1,0:T(8,128)(2,1)S(1)} %fold.14.rest_0_), channel_id=1, source_target_pairs={{0,0},{1,8},{2,16},{3,24},{4,4},{5,12},{6,20},{7,28},{8,1},{9,9},{... | collective-permute-start | bytes 393224 | tf_op jit(solution)/shard_map/ppermute | solution.py:268
  122.9 14.5 %collective-permute-start.39 = (bf16[256,256]{1,0:T(8,128)(2,1)S(1)}, bf16[256,256]{1,0:T(8,128)(2,1)S(1)}, u32[]{:S(2)}, u32[]{:S(2)}) collective-permute-start(bf16[256,256]{1,0:T(8,128)(2,1)S(1)} %fold.23.rest_0_), channel_id=1, source_target_pairs={{0,1},{1,0},{2,3},{3,2},{4,5},{5,4},{6,7},{7,6},{8,9},{9,8},{10,11... | collective-permute-start | bytes 393224 | tf_op jit(solution)/shard_map/ppermute | solution.py:268
  127.3 12.7 %collective-permute-start.40 = (bf16[256,256]{1,0:T(8,128)(2,1)S(1)}, bf16[256,256]{1,0:T(8,128)(2,1)S(1)}, u32[]{:S(2)}, u32[]{:S(2)}) collective-permute-start(bf16[256,256]{1,0:T(8,128)(2,1)S(1)} %fold.23.rest_0_), channel_id=1, source_target_pairs={{0,2},{1,3},{2,0},{3,1},{4,6},{5,7},{6,4},{7,5},{8,10},{9,11},{10,... | collective-permute-start | bytes 393224 | tf_op jit(solution)/shard_map/ppermute | solution.py:268
  134.7 9.0 %collective-permute-start.41 = (bf16[256,256]{1,0:T(8,128)(2,1)S(1)}, bf16[256,256]{1,0:T(8,128)(2,1)S(1)}, u32[]{:S(2)}, u32[]{:S(2)}) collective-permute-start(bf16[256,256]{1,0:T(8,128)(2,1)S(1)} %fold.23.rest_0_), channel_id=1, source_target_pairs={{0,3},{1,2},{2,1},{3,0},{4,7},{5,6},{6,5},{7,4},{8,11},{9,10},{10,... | collective-permute-start | bytes 393224 | tf_op jit(solution)/shard_map/ppermute | solution.py:268
  134.8 18.6 %collective-permute-start.35 = (bf16[4,256,256]{2,1,0:T(8,128)(2,1)S(1)}, bf16[4,256,256]{2,1,0:T(8,128)(2,1)S(1)}, u32[]{:S(2)}, u32[]{:S(2)}) collective-permute-start(bf16[4,256,256]{2,1,0:T(8,128)(2,1)S(1)} %stack.14.rest_4_), channel_id=1, source_target_pairs={{0,4},{1,5},{2,6},{3,7},{4,0},{5,1},{6,2},{7,3},{8,12},{9,13},{10,... | collective-permute-start | bytes 1572872 | tf_op jit(solution)/shard_map/ppermute | solution.py:268
  137.4 14.1 %collective-permute-start.28 = (bf16[256,256]{1,0:T(8,128)(2,1)S(1)}, bf16[256,256]{1,0:T(8,128)(2,1)S(1)}, u32[]{:S(2)}, u32[]{:S(2)}) collective-permute-start(bf16[256,256]{1,0:T(8,128)(2,1)S(1)} %fold.20.rest_0_), channel_id=1, source_target_pairs={{0,1},{1,0},{2,3},{3,2},{4,5},{5,4},{6,7},{7,6},{8,9},{9,8},{10,11... | collective-permute-start | bytes 393224 | tf_op jit(solution)/shard_map/ppermute | solution.py:268
  140.0 11.6 %collective-permute-start.29 = (bf16[256,256]{1,0:T(8,128)(2,1)S(1)}, bf16[256,256]{1,0:T(8,128)(2,1)S(1)}, u32[]{:S(2)}, u32[]{:S(2)}) collective-permute-start(bf16[256,256]{1,0:T(8,128)(2,1)S(1)} %fold.20.rest_0_), channel_id=1, source_target_pairs={{0,2},{1,3},{2,0},{3,1},{4,6},{5,7},{6,4},{7,5},{8,10},{9,11},{10,... | collective-permute-start | bytes 393224 | tf_op jit(solution)/shard_map/ppermute | solution.py:268
  143.6 8.0 %collective-permute-start.30 = (bf16[256,256]{1,0:T(8,128)(2,1)S(1)}, bf16[256,256]{1,0:T(8,128)(2,1)S(1)}, u32[]{:S(2)}, u32[]{:S(2)}) collective-permute-start(bf16[256,256]{1,0:T(8,128)(2,1)S(1)} %fold.20.rest_0_), channel_id=1, source_target_pairs={{0,3},{1,2},{2,1},{3,0},{4,7},{5,6},{6,5},{7,4},{8,11},{9,10},{10,... | collective-permute-start | bytes 393224 | tf_op jit(solution)/shard_map/ppermute | solution.py:268
  144.4 17.8 %collective-permute-start.24 = (bf16[4,256,256]{2,1,0:T(8,128)(2,1)S(1)}, bf16[4,256,256]{2,1,0:T(8,128)(2,1)S(1)}, u32[]{:S(2)}, u32[]{:S(2)}) collective-permute-start(bf16[4,256,256]{2,1,0:T(8,128)(2,1)S(1)} %stack.13.rest_4_), channel_id=1, source_target_pairs={{0,4},{1,5},{2,6},{3,7},{4,0},{5,1},{6,2},{7,3},{8,12},{9,13},{10,... | collective-permute-start | bytes 1572872 | tf_op jit(solution)/shard_map/ppermute | solution.py:268
  151.5 8.5 %collective-permute-start.17 = (bf16[256,256]{1,0:T(8,128)(2,1)S(1)}, bf16[256,256]{1,0:T(8,128)(2,1)S(1)}, u32[]{:S(2)}, u32[]{:S(2)}) collective-permute-start(bf16[256,256]{1,0:T(8,128)(2,1)S(1)} %fold.17.rest_0_), channel_id=1, source_target_pairs={{0,1},{1,0},{2,3},{3,2},{4,5},{5,4},{6,7},{7,6},{8,9},{9,8},{10,11... | collective-permute-start | bytes 393224 | tf_op jit(solution)/shard_map/ppermute | solution.py:268
  151.6 8.6 %collective-permute-start.18 = (bf16[256,256]{1,0:T(8,128)(2,1)S(1)}, bf16[256,256]{1,0:T(8,128)(2,1)S(1)}, u32[]{:S(2)}, u32[]{:S(2)}) collective-permute-start(bf16[256,256]{1,0:T(8,128)(2,1)S(1)} %fold.17.rest_0_), channel_id=1, source_target_pairs={{0,2},{1,3},{2,0},{3,1},{4,6},{5,7},{6,4},{7,5},{8,10},{9,11},{10,... | collective-permute-start | bytes 393224 | tf_op jit(solution)/shard_map/ppermute | solution.py:268
  151.7 9.9 %collective-permute-start.19 = (bf16[256,256]{1,0:T(8,128)(2,1)S(1)}, bf16[256,256]{1,0:T(8,128)(2,1)S(1)}, u32[]{:S(2)}, u32[]{:S(2)}) collective-permute-start(bf16[256,256]{1,0:T(8,128)(2,1)S(1)} %fold.17.rest_0_), channel_id=1, source_target_pairs={{0,3},{1,2},{2,1},{3,0},{4,7},{5,6},{6,5},{7,4},{8,11},{9,10},{10,... | collective-permute-start | bytes 393224 | tf_op jit(solution)/shard_map/ppermute | solution.py:268
  153.4 15.0 %collective-permute-start.6 = (bf16[256,256]{1,0:T(8,128)(2,1)S(1)}, bf16[256,256]{1,0:T(8,128)(2,1)S(1)}, u32[]{:S(2)}, u32[]{:S(2)}) collective-permute-start(bf16[256,256]{1,0:T(8,128)(2,1)S(1)} %fold.14.rest_0_), channel_id=1, source_target_pairs={{0,1},{1,0},{2,3},{3,2},{4,5},{5,4},{6,7},{7,6},{8,9},{9,8},{10,11... | collective-permute-start | bytes 393224 | tf_op jit(solution)/shard_map/ppermute | solution.py:268
  160.0 8.5 %collective-permute-start.7 = (bf16[256,256]{1,0:T(8,128)(2,1)S(1)}, bf16[256,256]{1,0:T(8,128)(2,1)S(1)}, u32[]{:S(2)}, u32[]{:S(2)}) collective-permute-start(bf16[256,256]{1,0:T(8,128)(2,1)S(1)} %fold.14.rest_0_), channel_id=1, source_target_pairs={{0,2},{1,3},{2,0},{3,1},{4,6},{5,7},{6,4},{7,5},{8,10},{9,11},{10,... | collective-permute-start | bytes 393224 | tf_op jit(solution)/shard_map/ppermute | solution.py:268
  160.1 8.3 %collective-permute-start.8 = (bf16[256,256]{1,0:T(8,128)(2,1)S(1)}, bf16[256,256]{1,0:T(8,128)(2,1)S(1)}, u32[]{:S(2)}, u32[]{:S(2)}) collective-permute-start(bf16[256,256]{1,0:T(8,128)(2,1)S(1)} %fold.14.rest_0_), channel_id=1, source_target_pairs={{0,3},{1,2},{2,1},{3,0},{4,7},{5,6},{6,5},{7,4},{8,11},{9,10},{10,... | collective-permute-start | bytes 393224 | tf_op jit(solution)/shard_map/ppermute | solution.py:268
  161.5 14.5 %collective-permute-start.13 = (bf16[4,256,256]{2,1,0:T(8,128)(2,1)S(1)}, bf16[4,256,256]{2,1,0:T(8,128)(2,1)S(1)}, u32[]{:S(2)}, u32[]{:S(2)}) collective-permute-start(bf16[4,256,256]{2,1,0:T(8,128)(2,1)S(1)} %stack.12.rest_4_), channel_id=1, source_target_pairs={{0,4},{1,5},{2,6},{3,7},{4,0},{5,1},{6,2},{7,3},{8,12},{9,13},{10,... | collective-permute-start | bytes 1572872 | tf_op jit(solution)/shard_map/ppermute | solution.py:268
  (3 other events, 42.0 us)

commit v2 on v1

v2 whole, which is shorter than its diff:
```python
import functools

import jax
import jax.numpy as jnp
from jax import lax
from jax.experimental import pallas as pl
from jax.experimental.pallas import tpu as pltpu
from jax.sharding import PartitionSpec as P

BATCH = 256
NBATCH = 4
AXES = ("pw", "band")
VMEM = pl.BlockSpec(memory_space=pltpu.VMEM)


def weigh(gap_row, frequencies, pair_total):
    return (
        -4.0 / pair_total * gap_row[None, :] / (gap_row[None, :] ** 2 + frequencies[:, None] ** 2)
    )


def scale_rows(weights, own_rows):
    return (weights[:, None, :] * own_rows.astype(jnp.float32)[None, :, :]).astype(jnp.bfloat16)


def plain_on_device(basis_set, densities, pair_gaps, frequencies):
    basis_width = basis_set.shape[1]
    pw_count = lax.axis_size("pw")
    band_count = lax.axis_size("band")
    row_share = basis_width // pw_count
    pair_total = pair_gaps.shape[0] * band_count
    nfreq = frequencies.shape[0]
    accumulated = jnp.zeros((nfreq, row_share, basis_width // band_count), jnp.float32)
    all_gaps = lax.all_gather(pair_gaps.reshape(NBATCH, BATCH), "band", axis=1, tiled=True)
    collected = []
    for position in range(NBATCH):
        dens_block = densities[:, position * BATCH : (position + 1) * BATCH]
        own_rows = lax.psum_scatter(
            lax.dot_general(
                basis_set, dens_block, (((0,), (0,)), ((), ())), preferred_element_type=jnp.float32
            ),
            "pw",
            scatter_dimension=0,
            tiled=True,
        ).astype(jnp.bfloat16)
        gathered = lax.all_gather(own_rows, "pw", axis=0, tiled=True)
        collected.append(own_rows)
        columns = lax.all_to_all(gathered, "band", split_axis=0, concat_axis=1, tiled=True)
        rows_all = lax.all_gather(own_rows, "band", axis=1, tiled=True)
        scaled = scale_rows(weigh(all_gaps[position], frequencies, pair_total), rows_all)
        accumulated = accumulated + jnp.einsum(
            "krp,cp->krc", scaled, columns, preferred_element_type=jnp.float32
        )
    projected = jnp.concatenate(collected, axis=1)
    return (accumulated, projected)


def project_kernel(me, dens_ref, basis_ref, out, *flipped, offset, masks, sent):
    count, rows, width = out.shape
    if flipped:
        flipped[0][...] = dens_ref[:, offset : offset + width].T
        dens_ref = flipped[0]
    for step in range(count):
        away = (step % 2) * masks[1] + (step // 2) * masks[2] + (masks[0] if sent else 0)
        block = jnp.bitwise_xor(me[0], away)
        part = jnp.dot(
            dens_ref[...],
            basis_ref[:, pl.ds(pl.multiple_of(block * rows, rows), rows)],
            preferred_element_type=jnp.float32,
        )
        out[step] = part.T.astype(out.dtype)


def project(me, dens, basis, offset, width, rows, masks, sent):
    depth = basis.shape[0]
    count = basis.shape[1] // rows // 2
    shapes = [(count, rows, width)] + ([(width, depth)] if sent else [])
    return pl.pallas_call(
        functools.partial(project_kernel, offset=offset, masks=masks, sent=sent),
        grid_spec=pltpu.PrefetchScalarGridSpec(
            num_scalar_prefetch=1,
            grid=(1,),
            in_specs=[VMEM] * 2,
            out_specs=[VMEM] * len(shapes),
        ),
        out_shape=[jax.ShapeDtypeStruct(shape, jnp.bfloat16) for shape in shapes],
        cost_estimate=pl.CostEstimate(
            flops=2 * depth * width * rows * count, bytes_accessed=0, transcendentals=0
        ),
        compiler_params=pltpu.CompilerParams(vmem_limit_bytes=12 << 20),
        name="project",
    )(me, dens, basis)


def fold_kernel(kept_ref, got_ref, *outs):
    for i in range(kept_ref.shape[0]):
        total = (kept_ref[i].astype(jnp.float32) + got_ref[i].astype(jnp.float32)).astype(
            jnp.bfloat16
        )
        if kept_ref.shape[0] == 1:
            outs[0][...] = total
        else:
            outs[i % 2][i // 2] = total


def fold(kept, got):
    count, rows, width = kept.shape
    if count == 1:
        shapes = [jax.ShapeDtypeStruct((rows, width), jnp.bfloat16)]
    else:
        shapes = [jax.ShapeDtypeStruct((count // 2, rows, width), jnp.bfloat16)] * 2
    return pl.pallas_call(
        fold_kernel,
        in_specs=[VMEM] * 2,
        out_specs=[VMEM] * len(shapes),
        out_shape=shapes,
        cost_estimate=pl.CostEstimate(
            flops=count * rows * width, bytes_accessed=4 * count * rows * width, transcendentals=0
        ),
        compiler_params=pltpu.CompilerParams(vmem_limit_bytes=8 << 20),
        name="fold",
    )(kept, got)


def join_kernel(*refs):
    offset = 0
    for ref in refs[:-1]:
        if len(ref.shape) == 2:
            refs[-1][offset] = ref[...]
            offset += 1
        else:
            refs[-1][offset : offset + ref.shape[0]] = ref[...]
            offset += ref.shape[0]


def join(*pieces):
    rows, width = pieces[0].shape[-2:]
    count = sum(1 if p.ndim == 2 else p.shape[0] for p in pieces)
    return pl.pallas_call(
        join_kernel,
        in_specs=[VMEM] * len(pieces),
        out_specs=VMEM,
        out_shape=jax.ShapeDtypeStruct((count, rows, width), jnp.bfloat16),
        cost_estimate=pl.CostEstimate(
            flops=rows * width, bytes_accessed=4 * rows * width, transcendentals=0
        ),
        compiler_params=pltpu.CompilerParams(vmem_limit_bytes=8 << 20),
        name="join",
    )(*pieces)


def align_kernel(me, band, a_ref, b_ref, out_ref):
    plane = me[0] // 2
    turned = jnp.bitwise_and(plane, 1) * 2 + plane // 2
    shift = jnp.bitwise_xor(turned, band[0])
    for i in range(4):
        ref = a_ref if i < 2 else b_ref
        out_ref[jnp.bitwise_xor(shift, i)] = ref[i % 2]


def align(me, band, a, b):
    shape = (2 * a.shape[0], *a.shape[1:])
    return pl.pallas_call(
        align_kernel,
        grid_spec=pltpu.PrefetchScalarGridSpec(
            num_scalar_prefetch=2, grid=(1,), in_specs=[VMEM] * 2, out_specs=VMEM
        ),
        out_shape=jax.ShapeDtypeStruct(shape, a.dtype),
        cost_estimate=pl.CostEstimate(
            flops=a.size, bytes_accessed=8 * a.size, transcendentals=0
        ),
        compiler_params=pltpu.CompilerParams(vmem_limit_bytes=8 << 20),
        name="align",
    )(me, band, a, b)


def sort_kernel(me, band, two_ref, got_ref, own_ref, keep_ref, send_ref):
    other = jnp.bitwise_and(jnp.bitwise_xor(me[0] // 2, band[0]), 1)
    count = keep_ref.shape[0]

    @pl.when(other == 0)
    def _():
        keep_ref[...] = two_ref[...]
        send_ref[:count] = got_ref[...]

    @pl.when(other != 0)
    def _():
        keep_ref[...] = got_ref[...]
        send_ref[:count] = two_ref[...]

    send_ref[count] = own_ref[...]


def sort(me, band, two, got, own):
    count, rows, width = two.shape
    return pl.pallas_call(
        sort_kernel,
        grid_spec=pltpu.PrefetchScalarGridSpec(
            num_scalar_prefetch=2, grid=(1,), in_specs=[VMEM] * 3, out_specs=[VMEM] * 2
        ),
        out_shape=[
            jax.ShapeDtypeStruct((count, rows, width), two.dtype),
            jax.ShapeDtypeStruct((count + 1, rows, width), two.dtype),
        ],
        cost_estimate=pl.CostEstimate(
            flops=two.size, bytes_accessed=8 * two.size, transcendentals=0
        ),
        compiler_params=pltpu.CompilerParams(vmem_limit_bytes=8 << 20),
        name="sort",
    )(me, band, two, got, own)


def split_kernel(me, band, keep_ref, got_ref, own_ref, near_ref, send_ref, rows_ref):
    mine = jnp.bitwise_xor(me[0] // 4, band[0] // 2)
    near_ref[0] = keep_ref[mine]
    near_ref[1] = got_ref[mine]
    send_ref[0] = keep_ref[1 - mine]
    send_ref[1] = got_ref[1 - mine]
    rows_ref[0] = own_ref[...]
    rows_ref[1] = got_ref[2]


def split(me, band, keep, got, own):
    shape = jax.ShapeDtypeStruct(keep.shape, keep.dtype)
    return pl.pallas_call(
        split_kernel,
        grid_spec=pltpu.PrefetchScalarGridSpec(
            num_scalar_prefetch=2, grid=(1,), in_specs=[VMEM] * 3, out_specs=[VMEM] * 3
        ),
        out_shape=[shape] * 3,
        cost_estimate=pl.CostEstimate(
            flops=keep.size, bytes_accessed=8 * keep.size, transcendentals=0
        ),
        compiler_params=pltpu.CompilerParams(vmem_limit_bytes=8 << 20),
        name="split",
    )(me, band, keep, got, own)


def respond_kernel(me, weights_ref, rows_ref, *rest, per_step, offset, halves, acc, last):
    cols_in = rest[: len(halves)]
    rest = rest[len(halves) :]
    acc_ref = rest[0] if acc else None
    out_ref, scaled_s = rest[-2:]
    planes, rows, width = rows_ref.shape
    step = pl.program_id(0)
    side = jnp.bitwise_and(me[0], 1)
    for k in range(planes):
        base = rows_ref[k].astype(jnp.float32)
        for f in range(per_step):
            w = weights_ref[k, pl.ds(step * per_step + f, 1), offset : offset + width]
            scaled_s[f * rows : (f + 1) * rows, k * width : (k + 1) * width] = (w * base).astype(
                jnp.bfloat16
            )
    here = pl.ds(step * per_step, per_step)
    for cols, far in zip(cols_in, halves):
        total = None
        for k in range(planes):
            part = lax.dot_general(
                scaled_s[:, k * width : (k + 1) * width],
                cols[k],
                (((1,), (1,)), ((), ())),
                preferred_element_type=jnp.float32,
            )
            total = part if total is None else total + part
        total = total.reshape(per_step, rows, rows)
        half = 1 - side if far else side
        where = pl.ds(pl.multiple_of(half * rows, rows), rows)
        if acc:
            total = total + acc_ref[here, :, where]
        if last:
            out_ref[...] = total
        else:
            out_ref[here, :, where] = total


def respond(me, weights, rows_in, cols_in, halves, acc, offset, last=False, onto=None):
    planes, rows, width = rows_in.shape
    nfreq = weights.shape[1]
    per_step = 4
    args = [weights, rows_in, *cols_in]
    in_specs = [VMEM] * len(args)
    aliases = {}
    if acc is not None:
        args.append(acc)
        in_specs.append(VMEM)
        if not last:
            aliases = {len(args): 0}
    if onto is not None:
        args.append(onto)
        in_specs.append(pl.BlockSpec(memory_space=pl.ANY))
        aliases = {len(args): 0}
    if last:
        far = int(halves[0])
        out_spec = pl.BlockSpec(
            (per_step, rows, rows),
            lambda step, me: (step, 0, jnp.bitwise_xor(jnp.bitwise_and(me[0], 1), far)),
        )
    else:
        out_spec = VMEM
    return pl.pallas_call(
        functools.partial(
            respond_kernel,
            per_step=per_step,
            offset=offset,
            halves=halves,
            acc=acc is not None,
            last=last,
        ),
        grid_spec=pltpu.PrefetchScalarGridSpec(
            num_scalar_prefetch=1,
            grid=(nfreq // per_step,),
            in_specs=in_specs,
            out_specs=out_spec,
            scratch_shapes=[pltpu.VMEM((per_step * rows, planes * width), jnp.bfloat16)],
        ),
        out_shape=jax.ShapeDtypeStruct((nfreq, rows, 2 * rows), jnp.float32),
        input_output_aliases=aliases,
        cost_estimate=pl.CostEstimate(
            flops=2 * nfreq * rows * rows * len(halves) * planes * width,
            bytes_accessed=nfreq * rows * 2 * rows * 4,
            transcendentals=0,
        ),
        compiler_params=pltpu.CompilerParams(
            dimension_semantics=("arbitrary",), vmem_limit_bytes=20 << 20
        ),
        name="respond",
    )(me, *args)


def grid_on_device(basis_set, densities, pair_gaps, frequencies):
    planes = lax.axis_size("band")
    rows = basis_set.shape[1] // lax.axis_size("pw")
    pairs = densities.shape[1]
    unit = pairs // sum(SHARES)
    widths = [share * unit for share in SHARES]
    offsets = [start * unit for start in STARTS]

    def permute(value, move):
        pairs_of = []
        for z in range(planes):
            for x in range(2):
                for b in range(planes):
                    to = move(z, x, b)
                    if to is not None:
                        tz, tx, tb = to
                        pairs_of.append(((z * 2 + x) * planes + b, (tz * 2 + tx) * planes + tb))
        return lax.ppermute(value, AXES, pairs_of)

    def across(mask):
        return lambda z, x, b: (z ^ (mask // 2), x ^ (mask % 2), b)

    me = lax.axis_index("pw").astype(jnp.int32).reshape(1)
    band = lax.axis_index("band").astype(jnp.int32).reshape(1)

    away, kept = [], []
    for at, width, masks in zip(offsets, widths, MASKS):
        out, flipped = project(
            me, densities, basis_set, at, width, rows, masks, True
        )
        away.append(out)
        kept += project(me, flipped, basis_set, 0, width, rows, masks, False)
    gaps = [pair_gaps.reshape(-1, 128)]
    for d in range(1, planes):
        gaps.append(permute(gaps[0], lambda z, x, b, d=d: (z, x, b ^ d)))
    weights = jnp.stack(
        [weigh(g.reshape(-1), frequencies, pairs * planes) for g in gaps]
    )

    acc = None
    collected = []
    for i in range(len(widths)):
        masks = MASKS[i]
        got = permute(away[i], across(masks[0]))
        held, sent = fold(kept[i], got)
        got = permute(sent, across(masks[1]))
        held, sent = fold(held, got)
        got = permute(sent, across(masks[2]))
        (own,) = fold(held, got)
        collected.append(own)
        if DIRECT[i]:
            got = permute(own, lambda z, x, b: (z, x, b ^ 1))
            two = join(own, got)
            got = permute(two, lambda z, x, b: (z, x, b ^ 2))
            rows_in = join(two, got)
            got = [
                permute(two, lambda z, x, b, m=m: (b % 2 * 2 + ((b // 2) ^ m), x, z))
                for m in range(2)
            ]
            near = align(me, band, *got)
        else:
            got = permute(own, across(4))
            two = join(own, got)
            got = permute(two, across(2))
            keep, send = sort(me, band, two, got, own)
            got = permute(send, lambda z, x, b: (z, x, b ^ 1))
            near, send, two = split(me, band, keep, got, own)
            got = permute(send, lambda z, x, b: (z, x, b ^ 2))
            near = join(near, got)
            got = permute(two, lambda z, x, b: (z, x, b ^ 2))
            rows_in = join(two, got)
        far = permute(near, across(1))
        if i < len(widths) - 1:
            acc = respond(
                me, weights, rows_in, [near, far], (False, True), acc, offsets[i]
            )
        else:
            half = respond(
                me, weights, rows_in, [near], (False,), acc, offsets[i], True
            )
            acc = respond(
                me, weights, rows_in, [far], (True,), acc, offsets[i], True, half
            )
    in_place = sorted(range(len(widths)), key=lambda i: offsets[i])
    return (acc, jnp.concatenate([collected[i] for i in in_place], axis=1))


SHARES = (2, 2, 2, 2)
STARTS = (0, 2, 4, 6)
MASKS = ((1, 2, 4), (1, 2, 4), (1, 2, 4), (1, 2, 4))
DIRECT = (True, True, True, True)


def solution(mesh):
    planes = mesh.shape["band"]
    on_grid = mesh.shape["pw"] == 2 * planes and planes == 4
    in_specs = (P("pw", None), P("pw", "band"), P("band"), P())
    out_specs = (P(None, "pw", "band"), P("pw", "band"))
    return jax.shard_map(
        grid_on_device if on_grid else plain_on_device,
        mesh=mesh,
        in_specs=in_specs,
        out_specs=out_specs,
        check_vma=False,
    )
```

time: 181 us -> 182 us (level)
  waiting for transfers between devices: 33.5 us -> 64.1 us
  starting transfers between devices: 89.4 us -> 64.1 us
  Pallas kernels: 48.8 us -> 43.8 us
    ppermute x47 -> x35, waiting for transfers between devices: 33.5 us -> 64.1 us  [permute(): return lax.ppermute(value, AXES, pairs_of)]
    ppermute x47 -> x35, starting transfers between devices: 89.4 us -> 64.1 us  [permute(): return lax.ppermute(value, AXES, pairs_of)]
    pallas_call x13 -> x25, Pallas kernels: 47.9 us -> 42.9 us  [the longest x5 26.5 us: respond(): pl.pallas_call(functools.partial(respond_kernel, per_step=per_step, offse...]
    unnamed x8 -> x14, local copies, waits for them, and re-layouts: 7.37 us -> 7.38 us
  transfers between devices with their start and end apart: 47 -> 35, of which waited for: 7 -> 15; matrix products, arithmetic and copies ran while one was open for 1% -> 1% of each run, Pallas kernels for 22% -> 21%
where the time goes in v2:
time: 182 us; the launch traced here: 181 us
  starting transfers between devices  64.1 us (35%)
  waiting for transfers between devices  64.1 us (35%)
  Pallas kernels  43.8 us (24%)
  local copies, waits for them, and re-layouts  7.38 us (4%)
    ppermute x35, starting transfers between devices, permute(): return lax.ppermute(value, AXES, pairs_of)  64.1 us
    ppermute x35, waiting for transfers between devices, permute(): return lax.ppermute(value, AXES, pairs_of)  64.1 us
    pallas_call x5, Pallas kernels, respond(): pl.pallas_call(functools.partial(respond_kernel, per_step=per_step, offse...  26.5 us
    pallas_call x8, Pallas kernels, project(): pl.pallas_call(functools.partial(project_kernel, offset=offset, masks=mas...  16 us
    unnamed x14, local copies, waits for them, and re-layouts  7.38 us
  transfers between devices with their start and end apart: 35, of which 15 were waited for; matrix products, arithmetic and copies ran while one was open for 1% of the time, Pallas kernels for 21%

profile of v2, /device:TPU:0, one launch (start us, length us, event | category | flops | bytes accessed | tf_op | source)
XLA Modules:
  0.0 181.4 jit_solution(18124401544527024001)
XLA Ops:
  0.6 4.6 %copy-done = bf16[3072,2048]{1,0:T(8,128)(2,1)S(1)} copy-done((bf16[3072,2048]{1,0:T(8,128)(2,1)S(1)}, bf16[3072,2048]{1,0:T(8,128)(2,1)}, u32[]{:S(2)}) %copy-start) | copy-done | bytes 12582936
  5.2 2.8 %copy-done.1 = bf16[3072,1024]{1,0:T(8,128)(2,1)S(1)} copy-done((bf16[3072,1024]{1,0:T(8,128)(2,1)S(1)}, bf16[3072,1024]{1,0:T(8,128)(2,1)}, u32[]{:S(2)}) %copy-start.1) | copy-done | bytes 6291480
  8.0 2.0 %project.10 = (bf16[4,256,256]{2,1,0:T(8,128)(2,1)S(1)}, bf16[256,3072]{1,0:T(8,128)(2,1)S(1)}) custom-call(s32[1]{0:T(128)} %bitcast.me, bf16[3072,1024]{1,0:T(8,128)(2,1)S(1)} %copy-done.1, bf16[3072,2048]{1,0:T(8,128)(2,1)S(1)} %copy-done), custom_call_target="tpu_custom_call" | custom-call | flops 1610612736 | tf_op jit(solution)/shard_map/project/pallas_call | solution.py:78
  10.0 3.1 %collective-permute-start.11 = (bf16[4,256,256]{2,1,0:T(8,128)(2,1)S(1)}, bf16[4,256,256]{2,1,0:T(8,128)(2,1)S(1)}, u32[]{:S(2)}, u32[]{:S(2)}) collective-permute-start(bf16[4,256,256]{2,1,0:T(8,128)(2,1)S(1)} %get-tuple-element.33), channel_id=1, source_target_pairs={{0,4},{1,5},{2,6},{3,7},{4,0},{5,1},{6,2},{7,3},{8,12},{9,13},{10,... | collective-permute-start | bytes 1572872 | tf_op jit(solution)/shard_map/ppermute | solution.py:347
  13.0 2.0 %project.8 = (bf16[4,256,256]{2,1,0:T(8,128)(2,1)S(1)}, bf16[256,3072]{1,0:T(8,128)(2,1)S(1)}) custom-call(s32[1]{0:T(128)} %bitcast.me, bf16[3072,1024]{1,0:T(8,128)(2,1)S(1)} %copy-done.1, bf16[3072,2048]{1,0:T(8,128)(2,1)S(1)} %copy-done), custom_call_target="tpu_custom_call" | custom-call | flops 1610612736 | tf_op jit(solution)/shard_map/project/pallas_call | solution.py:78
  15.2 2.0 %project.14 = (bf16[4,256,256]{2,1,0:T(8,128)(2,1)S(1)}, bf16[256,3072]{1,0:T(8,128)(2,1)S(1)}) custom-call(s32[1]{0:T(128)} %bitcast.me, bf16[3072,1024]{1,0:T(8,128)(2,1)S(1)} %copy-done.1, bf16[3072,2048]{1,0:T(8,128)(2,1)S(1)} %copy-done), custom_call_target="tpu_custom_call" | custom-call | flops 1610612736 | tf_op jit(solution)/shard_map/project/pallas_call | solution.py:78
  17.2 2.0 %collective-permute-start.27 = (bf16[4,256,256]{2,1,0:T(8,128)(2,1)S(1)}, bf16[4,256,256]{2,1,0:T(8,128)(2,1)S(1)}, u32[]{:S(2)}, u32[]{:S(2)}) collective-permute-start(bf16[4,256,256]{2,1,0:T(8,128)(2,1)S(1)} %get-tuple-element.45), channel_id=1, source_target_pairs={{0,4},{1,5},{2,6},{3,7},{4,0},{5,1},{6,2},{7,3},{8,12},{9,13},{10,... | collective-permute-start | bytes 1572872 | tf_op jit(solution)/shard_map/ppermute | solution.py:347
  19.2 2.0 %project.12 = (bf16[4,256,256]{2,1,0:T(8,128)(2,1)S(1)}, bf16[256,3072]{1,0:T(8,128)(2,1)S(1)}) custom-call(s32[1]{0:T(128)} %bitcast.me, bf16[3072,1024]{1,0:T(8,128)(2,1)S(1)} %copy-done.1, bf16[3072,2048]{1,0:T(8,128)(2,1)S(1)} %copy-done), custom_call_target="tpu_custom_call" | custom-call | flops 1610612736 | tf_op jit(solution)/shard_map/project/pallas_call | solution.py:78
  21.4 1.9 %project.11.kept_ref = bf16[4,256,256]{2,1,0:T(8,128)(2,1)S(1)} custom-call(s32[1]{0:T(128)} %bitcast.me, bf16[256,3072]{1,0:T(8,128)(2,1)S(1)} %get-tuple-element.32.dens_ref, bf16[3072,2048]{1,0:T(8,128)(2,1)S(1)} %bitcast.16), custom_call_target="tpu_custom_call" | custom-call | flops 1610612736 | tf_op jit(solution)/shard_map/project/pallas_call | solution.py:78
  23.3 1.9 %project.9.kept_ref = bf16[4,256,256]{2,1,0:T(8,128)(2,1)S(1)} custom-call(s32[1]{0:T(128)} %bitcast.me, bf16[256,3072]{1,0:T(8,128)(2,1)S(1)} %get-tuple-element.26.dens_ref, bf16[3072,2048]{1,0:T(8,128)(2,1)S(1)} %bitcast.16), custom_call_target="tpu_custom_call" | custom-call | flops 1610612736 | tf_op jit(solution)/shard_map/project/pallas_call | solution.py:78
  25.3 1.9 %project.15.kept_ref = bf16[4,256,256]{2,1,0:T(8,128)(2,1)S(1)} custom-call(s32[1]{0:T(128)} %bitcast.me, bf16[256,3072]{1,0:T(8,128)(2,1)S(1)} %get-tuple-element.44.dens_ref, bf16[3072,2048]{1,0:T(8,128)(2,1)S(1)} %bitcast.16), custom_call_target="tpu_custom_call" | custom-call | flops 1610612736 | tf_op jit(solution)/shard_map/project/pallas_call | solution.py:78
  27.4 2.0 %collective-permute-start.12 = (bf16[2,256,256]{2,1,0:T(8,128)(2,1)S(1)}, bf16[2,256,256]{2,1,0:T(8,128)(2,1)S(1)}, u32[]{:S(2)}, u32[]{:S(2)}) collective-permute-start(bf16[2,256,256]{2,1,0:T(8,128)(2,1)S(1)} %get-tuple-element.35), channel_id=1, source_target_pairs={{0,8},{1,9},{2,10},{3,11},{4,12},{5,13},{6,14},{7,15},{8,0},{9,1},... | collective-permute-start | bytes 786440 | tf_op jit(solution)/shard_map/ppermute | solution.py:347
  29.3 7.7 %collective-permute-done.3.got_ref = bf16[4,256,256]{2,1,0:T(8,128)(2,1)S(1)} collective-permute-done((bf16[4,256,256]{2,1,0:T(8,128)(2,1)S(1)}, bf16[4,256,256]{2,1,0:T(8,128)(2,1)S(1)}, u32[]{:S(2)}, u32[]{:S(2)}) %collective-permute-start.3) | collective-permute-done | bytes 524320 | tf_op jit(solution)/shard_map/ppermute | solution.py:347
  37.2 2.1 %collective-permute-start.4 = (bf16[2,256,256]{2,1,0:T(8,128)(2,1)S(1)}, bf16[2,256,256]{2,1,0:T(8,128)(2,1)S(1)}, u32[]{:S(2)}, u32[]{:S(2)}) collective-permute-start(bf16[2,256,256]{2,1,0:T(8,128)(2,1)S(1)} %get-tuple-element.29), channel_id=1, source_target_pairs={{0,8},{1,9},{2,10},{3,11},{4,12},{5,13},{6,14},{7,15},{8,0},{9,1},... | collective-permute-start | bytes 786440 | tf_op jit(solution)/shard_map/ppermute | solution.py:347
  39.3 9.0 %collective-permute-done.27.got_ref = bf16[4,256,256]{2,1,0:T(8,128)(2,1)S(1)} collective-permute-done((bf16[4,256,256]{2,1,0:T(8,128)(2,1)S(1)}, bf16[4,256,256]{2,1,0:T(8,128)(2,1)S(1)}, u32[]{:S(2)}, u32[]{:S(2)}) %collective-permute-start.27) | collective-permute-done | bytes 524320 | tf_op jit(solution)/shard_map/ppermute | solution.py:347
  48.4 2.1 %collective-permute-start.28 = (bf16[2,256,256]{2,1,0:T(8,128)(2,1)S(1)}, bf16[2,256,256]{2,1,0:T(8,128)(2,1)S(1)}, u32[]{:S(2)}, u32[]{:S(2)}) collective-permute-start(bf16[2,256,256]{2,1,0:T(8,128)(2,1)S(1)} %get-tuple-element.47), channel_id=1, source_target_pairs={{0,8},{1,9},{2,10},{3,11},{4,12},{5,13},{6,14},{7,15},{8,0},{9,1},... | collective-permute-start | bytes 786440 | tf_op jit(solution)/shard_map/ppermute | solution.py:347
  50.5 2.1 %project.13.kept_ref = bf16[4,256,256]{2,1,0:T(8,128)(2,1)S(1)} custom-call(s32[1]{0:T(128)} %bitcast.me, bf16[256,3072]{1,0:T(8,128)(2,1)S(1)} %get-tuple-element.38.dens_ref, bf16[3072,2048]{1,0:T(8,128)(2,1)S(1)} %bitcast.16), custom_call_target="tpu_custom_call" | custom-call | flops 1610612736 | tf_op jit(solution)/shard_map/project/pallas_call | solution.py:78
  52.7 6.0 %collective-permute-done.19.got_ref = bf16[4,256,256]{2,1,0:T(8,128)(2,1)S(1)} collective-permute-done((bf16[4,256,256]{2,1,0:T(8,128)(2,1)S(1)}, bf16[4,256,256]{2,1,0:T(8,128)(2,1)S(1)}, u32[]{:S(2)}, u32[]{:S(2)}) %collective-permute-start.19) | collective-permute-done | bytes 524320 | tf_op jit(solution)/shard_map/ppermute | solution.py:347
  58.8 1.8 %collective-permute-start.20 = (bf16[2,256,256]{2,1,0:T(8,128)(2,1)S(1)}, bf16[2,256,256]{2,1,0:T(8,128)(2,1)S(1)}, u32[]{:S(2)}, u32[]{:S(2)}) collective-permute-start(bf16[2,256,256]{2,1,0:T(8,128)(2,1)S(1)} %get-tuple-element.41), channel_id=1, source_target_pairs={{0,8},{1,9},{2,10},{3,11},{4,12},{5,13},{6,14},{7,15},{8,0},{9,1},... | collective-permute-start | bytes 786440 | tf_op jit(solution)/shard_map/ppermute | solution.py:347
  60.7 2.7 %collective-permute-start.29 = (bf16[1,256,256]{2,1,0:T(8,128)(2,1)S(1)}, bf16[1,256,256]{2,1,0:T(8,128)(2,1)S(1)}, u32[]{:S(2)}, u32[]{:S(2)}) collective-permute-start(bf16[1,256,256]{2,1,0:T(8,128)(2,1)S(1)} %get-tuple-element.49), channel_id=1, source_target_pairs={{0,16},{1,17},{2,18},{3,19},{4,20},{5,21},{6,22},{7,23},{8,24},{9,... | collective-permute-start | bytes 393224 | tf_op jit(solution)/shard_map/ppermute | solution.py:347
  63.9 2.7 %collective-permute-start.5 = (bf16[1,256,256]{2,1,0:T(8,128)(2,1)S(1)}, bf16[1,256,256]{2,1,0:T(8,128)(2,1)S(1)}, u32[]{:S(2)}, u32[]{:S(2)}) collective-permute-start(bf16[1,256,256]{2,1,0:T(8,128)(2,1)S(1)} %get-tuple-element.31), channel_id=1, source_target_pairs={{0,16},{1,17},{2,18},{3,19},{4,20},{5,21},{6,22},{7,23},{8,24},{9,... | collective-permute-start | bytes 393224 | tf_op jit(solution)/shard_map/ppermute | solution.py:347
  66.6 4.3 %collective-permute-done.20.got_ref = bf16[2,256,256]{2,1,0:T(8,128)(2,1)S(1)} collective-permute-done((bf16[2,256,256]{2,1,0:T(8,128)(2,1)S(1)}, bf16[2,256,256]{2,1,0:T(8,128)(2,1)S(1)}, u32[]{:S(2)}, u32[]{:S(2)}) %collective-permute-start.20) | collective-permute-done | bytes 262176 | tf_op jit(solution)/shard_map/ppermute | solution.py:347
  70.9 1.4 collective-permute-start.21
  72.4 9.5 %collective-permute-done.13.got_ref = bf16[1,256,256]{2,1,0:T(8,128)(2,1)S(1)} collective-permute-done((bf16[1,256,256]{2,1,0:T(8,128)(2,1)S(1)}, bf16[1,256,256]{2,1,0:T(8,128)(2,1)S(1)}, u32[]{:S(2)}, u32[]{:S(2)}) %collective-permute-start.13) | collective-permute-done | bytes 131104 | tf_op jit(solution)/shard_map/ppermute | solution.py:347
  82.1 1.6 collective-permute-start.2
  83.7 1.1 collective-permute-done.5.got_ref
  84.8 1.5 collective-permute-start.1
  88.4 4.3 %collective-permute-start.17 = (bf16[2,256,256]{2,1,0:T(8,128)(2,1)S(1)}, bf16[2,256,256]{2,1,0:T(8,128)(2,1)S(1)}, u32[]{:S(2)}, u32[]{:S(2)}) collective-permute-start(bf16[2,256,256]{2,1,0:T(8,128)(2,1)S(1)} %join.10.refs_0_), channel_id=1, source_target_pairs={{0,8},{1,24},{2,0},{3,16},{4,12},{5,28},{6,4},{7,20},{8,9},{9,25},... | collective-permute-start | bytes 786440 | tf_op jit(solution)/shard_map/ppermute | solution.py:347
  94.5 2.7 %collective-permute-start.15 = (bf16[2,256,256]{2,1,0:T(8,128)(2,1)S(1)}, bf16[2,256,256]{2,1,0:T(8,128)(2,1)S(1)}, u32[]{:S(2)}, u32[]{:S(2)}) collective-permute-start(bf16[2,256,256]{2,1,0:T(8,128)(2,1)S(1)} %join.10.refs_0_), channel_id=1, source_target_pairs={{0,2},{1,3},{2,0},{3,1},{4,6},{5,7},{6,4},{7,5},{8,10},{9,11},{10,... | collective-permute-start | bytes 786440 | tf_op jit(solution)/shard_map/ppermute | solution.py:347
  97.2 2.1 %collective-permute-done.17.b_ref = bf16[2,256,256]{2,1,0:T(8,128)(2,1)S(1)} collective-permute-done((bf16[2,256,256]{2,1,0:T(8,128)(2,1)S(1)}, bf16[2,256,256]{2,1,0:T(8,128)(2,1)S(1)}, u32[]{:S(2)}, u32[]{:S(2)}) %collective-permute-start.17) | collective-permute-done | bytes 262176 | tf_op jit(solution)/shard_map/ppermute | solution.py:347
  99.4 2.5 %collective-permute-start.25 = (bf16[2,256,256]{2,1,0:T(8,128)(2,1)S(1)}, bf16[2,256,256]{2,1,0:T(8,128)(2,1)S(1)}, u32[]{:S(2)}, u32[]{:S(2)}) collective-permute-start(bf16[2,256,256]{2,1,0:T(8,128)(2,1)S(1)} %join.12.refs_0_), channel_id=1, source_target_pairs={{0,8},{1,24},{2,0},{3,16},{4,12},{5,28},{6,4},{7,20},{8,9},{9,25},... | collective-permute-start | bytes 786440 | tf_op jit(solution)/shard_map/ppermute | solution.py:347
  102.5 9.4 %collective-permute-start.9 = (bf16[2,256,256]{2,1,0:T(8,128)(2,1)S(1)}, bf16[2,256,256]{2,1,0:T(8,128)(2,1)S(1)}, u32[]{:S(2)}, u32[]{:S(2)}) collective-permute-start(bf16[2,256,256]{2,1,0:T(8,128)(2,1)S(1)} %join.8.refs_0_), channel_id=1, source_target_pairs={{0,8},{1,24},{2,0},{3,16},{4,12},{5,28},{6,4},{7,20},{8,9},{9,25},... | collective-permute-start | bytes 786440 | tf_op jit(solution)/shard_map/ppermute | solution.py:347
  112.0 1.6 collective-permute-start.34
  114.3 11.0 %collective-permute-done.9.b_ref = bf16[2,256,256]{2,1,0:T(8,128)(2,1)S(1)} collective-permute-done((bf16[2,256,256]{2,1,0:T(8,128)(2,1)S(1)}, bf16[2,256,256]{2,1,0:T(8,128)(2,1)S(1)}, u32[]{:S(2)}, u32[]{:S(2)}) %collective-permute-start.9) | collective-permute-done | bytes 262176 | tf_op jit(solution)/shard_map/ppermute | solution.py:347
  125.3 10.0 %collective-permute-start.7 = (bf16[2,256,256]{2,1,0:T(8,128)(2,1)S(1)}, bf16[2,256,256]{2,1,0:T(8,128)(2,1)S(1)}, u32[]{:S(2)}, u32[]{:S(2)}) collective-permute-start(bf16[2,256,256]{2,1,0:T(8,128)(2,1)S(1)} %join.8.refs_0_), channel_id=1, source_target_pairs={{0,2},{1,3},{2,0},{3,1},{4,6},{5,7},{6,4},{7,5},{8,10},{9,11},{10,... | collective-permute-start | bytes 786440 | tf_op jit(solution)/shard_map/ppermute | solution.py:347
  135.3 2.0 %collective-permute-start.23 = (bf16[2,256,256]{2,1,0:T(8,128)(2,1)S(1)}, bf16[2,256,256]{2,1,0:T(8,128)(2,1)S(1)}, u32[]{:S(2)}, u32[]{:S(2)}) collective-permute-start(bf16[2,256,256]{2,1,0:T(8,128)(2,1)S(1)} %join.12.refs_0_), channel_id=1, source_target_pairs={{0,2},{1,3},{2,0},{3,1},{4,6},{5,7},{6,4},{7,5},{8,10},{9,11},{10,... | collective-permute-start | bytes 786440 | tf_op jit(solution)/shard_map/ppermute | solution.py:347
  137.5 4.5 %collective-permute-done.7.refs_1_ = bf16[2,256,256]{2,1,0:T(8,128)(2,1)S(1)} collective-permute-done((bf16[2,256,256]{2,1,0:T(8,128)(2,1)S(1)}, bf16[2,256,256]{2,1,0:T(8,128)(2,1)S(1)}, u32[]{:S(2)}, u32[]{:S(2)}) %collective-permute-start.7) | collective-permute-done | bytes 262176 | tf_op jit(solution)/shard_map/ppermute | solution.py:347
  142.0 1.6 collective-permute-start.26
  145.1 2.0 %collective-permute-done.31.refs_1_ = bf16[2,256,256]{2,1,0:T(8,128)(2,1)S(1)} collective-permute-done((bf16[2,256,256]{2,1,0:T(8,128)(2,1)S(1)}, bf16[2,256,256]{2,1,0:T(8,128)(2,1)S(1)}, u32[]{:S(2)}, u32[]{:S(2)}) %collective-permute-start.31) | collective-permute-done | bytes 262176 | tf_op jit(solution)/shard_map/ppermute | solution.py:347
  147.1 1.4 collective-permute-start.10
  148.6 1.4 collective-permute-done.23.refs_1_
  150.0 5.5 %respond.5.rest_2_ = f32[16,256,512]{2,1,0:T(8,128)S(1)} custom-call(s32[1]{0:T(128)} %bitcast.me, f32[4,16,1024]{2,1,0:T(8,128)S(1)} %pad_maximum_fusion.1.weights_ref, bf16[4,256,256]{2,1,0:T(8,128)(2,1)S(1)} %join.15.rows_ref, bf16[4,256,256]{2,1,0:T(8,128)(2,1)S(1)} %align.7.rest_0_, bf16[4,256,256]{2,1,0:T(8,128)(2,1)S(1)} %collective-permute-done.34.rest_1_), custom_call_target="tpu_custom_call" | custom-call | flops 4294967296 | bytes 8388608 | tf_op jit(solution)/shard_map/respond/pallas_call | solution.py:300
  155.5 1.3 collective-permute-done.26.rest_1_
  156.8 6.3 %respond.6.rest_2_ = f32[16,256,512]{2,1,0:T(8,128)S(1)} custom-call(s32[1]{0:T(128)} %bitcast.me, f32[4,16,1024]{2,1,0:T(8,128)S(1)} %pad_maximum_fusion.1.weights_ref, bf16[4,256,256]{2,1,0:T(8,128)(2,1)S(1)} %join.13.rows_ref, bf16[4,256,256]{2,1,0:T(8,128)(2,1)S(1)} %align.6.rest_0_, ...), custom_call_target="tpu_custom_call", output_to_operand_aliasing={{}: (5, {})} | custom-call | flops 4294967296 | bytes 8388608 | tf_op jit(solution)/shard_map/respond/pallas_call | solution.py:300
  163.0 3.6 %collective-permute-done.18.rest_1_ = bf16[4,256,256]{2,1,0:T(8,128)(2,1)S(1)} collective-permute-done((bf16[4,256,256]{2,1,0:T(8,128)(2,1)S(1)}, bf16[4,256,256]{2,1,0:T(8,128)(2,1)S(1)}, u32[]{:S(2)}, u32[]{:S(2)}) %collective-permute-start.18) | collective-permute-done | bytes 524320 | tf_op jit(solution)/shard_map/ppermute | solution.py:347
  166.7 6.3 %respond.7.rest_1_ = f32[16,256,512]{2,1,0:T(8,128)S(1)} custom-call(s32[1]{0:T(128)} %bitcast.me, f32[4,16,1024]{2,1,0:T(8,128)S(1)} %pad_maximum_fusion.1.weights_ref, bf16[4,256,256]{2,1,0:T(8,128)(2,1)S(1)} %join.11.rows_ref, bf16[4,256,256]{2,1,0:T(8,128)(2,1)S(1)} %align.5.rest_0_, ...), custom_call_target="tpu_custom_call", output_to_operand_aliasing={{}: (5, {})} | custom-call | flops 4294967296 | bytes 8388608 | tf_op jit(solution)/shard_map/respond/pallas_call | solution.py:300
  172.9 4.2 %respond.8.rest_2_ = f32[16,256,512]{2,1,0:T(8,128)} custom-call(s32[1]{0:T(128)} %bitcast.me, f32[4,16,1024]{2,1,0:T(8,128)S(1)} %pad_maximum_fusion.1.weights_ref, bf16[4,256,256]{2,1,0:T(8,128)(2,1)S(1)} %join.9.rows_ref, bf16[4,256,256]{2,1,0:T(8,128)(2,1)S(1)} %align.4.rest_0_, f32[16,256,512]{2,1,0:T(8,128)S(1)} %respond.7.rest_1_), custom_call_target="tpu_custom_call" | custom-call | flops 2147483648 | bytes 8388608 | tf_op jit(solution)/shard_map/respond/pallas_call | solution.py:300
  177.2 4.2 %respond.9 = f32[16,256,512]{2,1,0:T(8,128)} custom-call(s32[1]{0:T(128)} %bitcast.me, f32[4,16,1024]{2,1,0:T(8,128)S(1)} %pad_maximum_fusion.1.weights_ref, bf16[4,256,256]{2,1,0:T(8,128)(2,1)S(1)} %join.9.rows_ref, bf16[4,256,256]{2,1,0:T(8,128)(2,1)S(1)} %collective-permute-done.10.rest_0_, ...), custom_call_target="tpu_custom_call", output_to_operand_aliasing={{}: (5, {})} | custom-call | flops 2147483648 | bytes 8388608 | tf_op jit(solution)/shard_map/respond/pallas_call | solution.py:300
  (82 shorter events, 8.7 us)
Async XLA Ops:
  0.6 4.6 %copy-start = (bf16[3072,2048]{1,0:T(8,128)(2,1)S(1)}, bf16[3072,2048]{1,0:T(8,128)(2,1)}, u32[]{:S(2)}) copy-start(bf16[3072,2048]{1,0:T(8,128)(2,1)} %basis_ref.15) | copy-start | bytes 37748740
  5.2 2.8 %copy-start.1 = (bf16[3072,1024]{1,0:T(8,128)(2,1)S(1)}, bf16[3072,1024]{1,0:T(8,128)(2,1)}, u32[]{:S(2)}) copy-start(bf16[3072,1024]{1,0:T(8,128)(2,1)} %dens_ref.7) | copy-start | bytes 18874372
  10.0 17.3 %collective-permute-start.11 = (bf16[4,256,256]{2,1,0:T(8,128)(2,1)S(1)}, bf16[4,256,256]{2,1,0:T(8,128)(2,1)S(1)}, u32[]{:S(2)}, u32[]{:S(2)}) collective-permute-start(bf16[4,256,256]{2,1,0:T(8,128)(2,1)S(1)} %get-tuple-element.33), channel_id=1, source_target_pairs={{0,4},{1,5},{2,6},{3,7},{4,0},{5,1},{6,2},{7,3},{8,12},{9,13},{10,... | collective-permute-start | bytes 1572872 | tf_op jit(solution)/shard_map/ppermute | solution.py:347
  15.1 22.0 %collective-permute-start.3 = (bf16[4,256,256]{2,1,0:T(8,128)(2,1)S(1)}, bf16[4,256,256]{2,1,0:T(8,128)(2,1)S(1)}, u32[]{:S(2)}, u32[]{:S(2)}) collective-permute-start(bf16[4,256,256]{2,1,0:T(8,128)(2,1)S(1)} %get-tuple-element.27), channel_id=1, source_target_pairs={{0,4},{1,5},{2,6},{3,7},{4,0},{5,1},{6,2},{7,3},{8,12},{9,13},{10,... | collective-permute-start | bytes 1572872 | tf_op jit(solution)/shard_map/ppermute | solution.py:347
  15.1 6.2 %slice-start = ((s8[12582912]{0:T(1024)(128)(4,1)}), s8[4194304]{0:T(1024)(128)(4,1)S(1)}, s32[]{:S(2)}) async-start(s8[12582912]{0:T(1024)(128)(4,1)} %bitcast.15), calls=%async_computation | async-start | bytes 8388608
  15.2 6.2 %slice-start.1 = ((s8[12582912]{0:T(1024)(128)(4,1)}), s8[4194304]{0:T(1024)(128)(4,1)S(1)}, s32[]{:S(2)}) async-start(s8[12582912]{0:T(1024)(128)(4,1)} %bitcast.15), calls=%async_computation.1 | async-start | bytes 8388608
  17.2 4.2 %slice-start.2 = ((s8[12582912]{0:T(1024)(128)(4,1)}), s8[4194304]{0:T(1024)(128)(4,1)S(1)}, s32[]{:S(2)}) async-start(s8[12582912]{0:T(1024)(128)(4,1)} %bitcast.15), calls=%async_computation.2 | async-start | bytes 8388608
  17.2 31.1 %collective-permute-start.27 = (bf16[4,256,256]{2,1,0:T(8,128)(2,1)S(1)}, bf16[4,256,256]{2,1,0:T(8,128)(2,1)S(1)}, u32[]{:S(2)}, u32[]{:S(2)}) collective-permute-start(bf16[4,256,256]{2,1,0:T(8,128)(2,1)S(1)} %get-tuple-element.45), channel_id=1, source_target_pairs={{0,4},{1,5},{2,6},{3,7},{4,0},{5,1},{6,2},{7,3},{8,12},{9,13},{10,... | collective-permute-start | bytes 1572872 | tf_op jit(solution)/shard_map/ppermute | solution.py:347
  21.3 37.4 %collective-permute-start.19 = (bf16[4,256,256]{2,1,0:T(8,128)(2,1)S(1)}, bf16[4,256,256]{2,1,0:T(8,128)(2,1)S(1)}, u32[]{:S(2)}, u32[]{:S(2)}) collective-permute-start(bf16[4,256,256]{2,1,0:T(8,128)(2,1)S(1)} %get-tuple-element.39), channel_id=1, source_target_pairs={{0,4},{1,5},{2,6},{3,7},{4,0},{5,1},{6,2},{7,3},{8,12},{9,13},{10,... | collective-permute-start | bytes 1572872 | tf_op jit(solution)/shard_map/ppermute | solution.py:347
  27.4 36.0 %collective-permute-start.12 = (bf16[2,256,256]{2,1,0:T(8,128)(2,1)S(1)}, bf16[2,256,256]{2,1,0:T(8,128)(2,1)S(1)}, u32[]{:S(2)}, u32[]{:S(2)}) collective-permute-start(bf16[2,256,256]{2,1,0:T(8,128)(2,1)S(1)} %get-tuple-element.35), channel_id=1, source_target_pairs={{0,8},{1,9},{2,10},{3,11},{4,12},{5,13},{6,14},{7,15},{8,0},{9,1},... | collective-permute-start | bytes 786440 | tf_op jit(solution)/shard_map/ppermute | solution.py:347
  37.2 26.7 %collective-permute-start.4 = (bf16[2,256,256]{2,1,0:T(8,128)(2,1)S(1)}, bf16[2,256,256]{2,1,0:T(8,128)(2,1)S(1)}, u32[]{:S(2)}, u32[]{:S(2)}) collective-permute-start(bf16[2,256,256]{2,1,0:T(8,128)(2,1)S(1)} %get-tuple-element.29), channel_id=1, source_target_pairs={{0,8},{1,9},{2,10},{3,11},{4,12},{5,13},{6,14},{7,15},{8,0},{9,1},... | collective-permute-start | bytes 786440 | tf_op jit(solution)/shard_map/ppermute | solution.py:347
  48.4 12.2 %collective-permute-start.28 = (bf16[2,256,256]{2,1,0:T(8,128)(2,1)S(1)}, bf16[2,256,256]{2,1,0:T(8,128)(2,1)S(1)}, u32[]{:S(2)}, u32[]{:S(2)}) collective-permute-start(bf16[2,256,256]{2,1,0:T(8,128)(2,1)S(1)} %get-tuple-element.47), channel_id=1, source_target_pairs={{0,8},{1,9},{2,10},{3,11},{4,12},{5,13},{6,14},{7,15},{8,0},{9,1},... | collective-permute-start | bytes 786440 | tf_op jit(solution)/shard_map/ppermute | solution.py:347
  50.5 31.5 %copy-start.2 = (f32[1024]{0:T(1024)S(1)}, f32[1024]{0:T(1024)}, u32[]{:S(2)}) copy-start(f32[1024]{0:T(1024)} %param.6) | copy-start | bytes 12292
  50.5 42.1 %copy-start.3 = (f32[16]{0:T(128)S(1)}, f32[16]{0:T(128)}, u32[]{:S(2)}) copy-start(f32[16]{0:T(128)} %param.7) | copy-start | bytes 196
  58.8 12.0 %collective-permute-start.20 = (bf16[2,256,256]{2,1,0:T(8,128)(2,1)S(1)}, bf16[2,256,256]{2,1,0:T(8,128)(2,1)S(1)}, u32[]{:S(2)}, u32[]{:S(2)}) collective-permute-start(bf16[2,256,256]{2,1,0:T(8,128)(2,1)S(1)} %get-tuple-element.41), channel_id=1, source_target_pairs={{0,8},{1,9},{2,10},{3,11},{4,12},{5,13},{6,14},{7,15},{8,0},{9,1},... | collective-permute-start | bytes 786440 | tf_op jit(solution)/shard_map/ppermute | solution.py:347
  60.7 11.6 %collective-permute-start.29 = (bf16[1,256,256]{2,1,0:T(8,128)(2,1)S(1)}, bf16[1,256,256]{2,1,0:T(8,128)(2,1)S(1)}, u32[]{:S(2)}, u32[]{:S(2)}) collective-permute-start(bf16[1,256,256]{2,1,0:T(8,128)(2,1)S(1)} %get-tuple-element.49), channel_id=1, source_target_pairs={{0,16},{1,17},{2,18},{3,19},{4,20},{5,21},{6,22},{7,23},{8,24},{9,... | collective-permute-start | bytes 393224 | tf_op jit(solution)/shard_map/ppermute | solution.py:347
  63.4 18.5 %collective-permute-start.13 = (bf16[1,256,256]{2,1,0:T(8,128)(2,1)S(1)}, bf16[1,256,256]{2,1,0:T(8,128)(2,1)S(1)}, u32[]{:S(2)}, u32[]{:S(2)}) collective-permute-start(bf16[1,256,256]{2,1,0:T(8,128)(2,1)S(1)} %get-tuple-element.37), channel_id=1, source_target_pairs={{0,16},{1,17},{2,18},{3,19},{4,20},{5,21},{6,22},{7,23},{8,24},{9,... | collective-permute-start | bytes 393224 | tf_op jit(solution)/shard_map/ppermute | solution.py:347
  63.9 20.9 %collective-permute-start.5 = (bf16[1,256,256]{2,1,0:T(8,128)(2,1)S(1)}, bf16[1,256,256]{2,1,0:T(8,128)(2,1)S(1)}, u32[]{:S(2)}, u32[]{:S(2)}) collective-permute-start(bf16[1,256,256]{2,1,0:T(8,128)(2,1)S(1)} %get-tuple-element.31), channel_id=1, source_target_pairs={{0,16},{1,17},{2,18},{3,19},{4,20},{5,21},{6,22},{7,23},{8,24},{9,... | collective-permute-start | bytes 393224 | tf_op jit(solution)/shard_map/ppermute | solution.py:347
  70.9 15.4 %collective-permute-start.21 = (bf16[1,256,256]{2,1,0:T(8,128)(2,1)S(1)}, bf16[1,256,256]{2,1,0:T(8,128)(2,1)S(1)}, u32[]{:S(2)}, u32[]{:S(2)}) collective-permute-start(bf16[1,256,256]{2,1,0:T(8,128)(2,1)S(1)} %get-tuple-element.43), channel_id=1, source_target_pairs={{0,16},{1,17},{2,18},{3,19},{4,20},{5,21},{6,22},{7,23},{8,24},{9,... | collective-permute-start | bytes 393224 | tf_op jit(solution)/shard_map/ppermute | solution.py:347
  72.4 14.1 %collective-permute-start.30 = (bf16[256,256]{1,0:T(8,128)(2,1)S(1)}, bf16[256,256]{1,0:T(8,128)(2,1)S(1)}, u32[]{:S(2)}, u32[]{:S(2)}) collective-permute-start(bf16[256,256]{1,0:T(8,128)(2,1)S(1)} %fold.23.refs_0_), channel_id=1, source_target_pairs={{0,1},{1,0},{2,3},{3,2},{4,5},{5,4},{6,7},{7,6},{8,9},{9,8},{10,11... | collective-permute-start | bytes 393224 | tf_op jit(solution)/shard_map/ppermute | solution.py:347
  82.0 5.1 %collective-permute-start.14 = (bf16[256,256]{1,0:T(8,128)(2,1)S(1)}, bf16[256,256]{1,0:T(8,128)(2,1)S(1)}, u32[]{:S(2)}, u32[]{:S(2)}) collective-permute-start(bf16[256,256]{1,0:T(8,128)(2,1)S(1)} %fold.17.refs_0_), channel_id=1, source_target_pairs={{0,1},{1,0},{2,3},{3,2},{4,5},{5,4},{6,7},{7,6},{8,9},{9,8},{10,11... | collective-permute-start | bytes 393224 | tf_op jit(solution)/shard_map/ppermute | solution.py:347
  82.1 5.1 %collective-permute-start.2 = (f32[8,128]{1,0:T(8,128)S(1)}, f32[8,128]{1,0:T(8,128)S(1)}, u32[]{:S(2)}, u32[]{:S(2)}) collective-permute-start(f32[8,128]{1,0:T(8,128)S(1)} %bitcast.17), channel_id=1, source_target_pairs={{0,3},{1,2},{2,1},{3,0},{4,7},{5,6},{6,5},{7,4},{8,11},{9,10},{10,... | collective-permute-start | bytes 12296 | tf_op jit(solution)/shard_map/ppermute | solution.py:347
  84.8 3.6 %collective-permute-start.1 = (f32[8,128]{1,0:T(8,128)S(1)}, f32[8,128]{1,0:T(8,128)S(1)}, u32[]{:S(2)}, u32[]{:S(2)}) collective-permute-start(f32[8,128]{1,0:T(8,128)S(1)} %bitcast.18), channel_id=1, source_target_pairs={{0,2},{1,3},{2,0},{3,1},{4,6},{5,7},{6,4},{7,5},{8,10},{9,11},{10,... | collective-permute-start | bytes 12296 | tf_op jit(solution)/shard_map/ppermute | solution.py:347
  86.3 6.3 %collective-permute-start.6 = (bf16[256,256]{1,0:T(8,128)(2,1)S(1)}, bf16[256,256]{1,0:T(8,128)(2,1)S(1)}, u32[]{:S(2)}, u32[]{:S(2)}) collective-permute-start(bf16[256,256]{1,0:T(8,128)(2,1)S(1)} %fold.14.refs_0_), channel_id=1, source_target_pairs={{0,1},{1,0},{2,3},{3,2},{4,5},{5,4},{6,7},{7,6},{8,9},{9,8},{10,11... | collective-permute-start | bytes 393224 | tf_op jit(solution)/shard_map/ppermute | solution.py:347
  86.5 7.2 %collective-permute-start.22 = (bf16[256,256]{1,0:T(8,128)(2,1)S(1)}, bf16[256,256]{1,0:T(8,128)(2,1)S(1)}, u32[]{:S(2)}, u32[]{:S(2)}) collective-permute-start(bf16[256,256]{1,0:T(8,128)(2,1)S(1)} %fold.20.refs_0_), channel_id=1, source_target_pairs={{0,1},{1,0},{2,3},{3,2},{4,5},{5,4},{6,7},{7,6},{8,9},{9,8},{10,11... | collective-permute-start | bytes 393224 | tf_op jit(solution)/shard_map/ppermute | solution.py:347
  87.0 14.8 %collective-permute-start.33 = (bf16[2,256,256]{2,1,0:T(8,128)(2,1)S(1)}, bf16[2,256,256]{2,1,0:T(8,128)(2,1)S(1)}, u32[]{:S(2)}, u32[]{:S(2)}) collective-permute-start(bf16[2,256,256]{2,1,0:T(8,128)(2,1)S(1)} %join.14.refs_0_), channel_id=1, source_target_pairs={{0,8},{1,24},{2,0},{3,16},{4,12},{5,28},{6,4},{7,20},{8,9},{9,25},... | collective-permute-start | bytes 786440 | tf_op jit(solution)/shard_map/ppermute | solution.py:347
  87.2 15.4 %collective-permute-start.32 = (bf16[2,256,256]{2,1,0:T(8,128)(2,1)S(1)}, bf16[2,256,256]{2,1,0:T(8,128)(2,1)S(1)}, u32[]{:S(2)}, u32[]{:S(2)}) collective-permute-start(bf16[2,256,256]{2,1,0:T(8,128)(2,1)S(1)} %join.14.refs_0_), channel_id=1, source_target_pairs={{0,0},{1,16},{2,8},{3,24},{4,4},{5,20},{6,12},{7,28},{8,1},{9,17},... | collective-permute-start | bytes 786440 | tf_op jit(solution)/shard_map/ppermute | solution.py:347
  88.4 11.0 %collective-permute-start.17 = (bf16[2,256,256]{2,1,0:T(8,128)(2,1)S(1)}, bf16[2,256,256]{2,1,0:T(8,128)(2,1)S(1)}, u32[]{:S(2)}, u32[]{:S(2)}) collective-permute-start(bf16[2,256,256]{2,1,0:T(8,128)(2,1)S(1)} %join.10.refs_0_), channel_id=1, source_target_pairs={{0,8},{1,24},{2,0},{3,16},{4,12},{5,28},{6,4},{7,20},{8,9},{9,25},... | collective-permute-start | bytes 786440 | tf_op jit(solution)/shard_map/ppermute | solution.py:347
  92.7 1.9 %collective-permute-start = (f32[8,128]{1,0:T(8,128)S(1)}, f32[8,128]{1,0:T(8,128)S(1)}, u32[]{:S(2)}, u32[]{:S(2)}) collective-permute-start(f32[8,128]{1,0:T(8,128)S(1)} %bitcast.19), channel_id=1, source_target_pairs={{0,1},{1,0},{2,3},{3,2},{4,5},{5,4},{6,7},{7,6},{8,9},{9,8},{10,11... | collective-permute-start | bytes 12296 | tf_op jit(solution)/shard_map/ppermute | solution.py:347
  93.7 18.3 %collective-permute-start.16 = (bf16[2,256,256]{2,1,0:T(8,128)(2,1)S(1)}, bf16[2,256,256]{2,1,0:T(8,128)(2,1)S(1)}, u32[]{:S(2)}, u32[]{:S(2)}) collective-permute-start(bf16[2,256,256]{2,1,0:T(8,128)(2,1)S(1)} %join.10.refs_0_), channel_id=1, source_target_pairs={{0,0},{1,16},{2,8},{3,24},{4,4},{5,20},{6,12},{7,28},{8,1},{9,17},... | collective-permute-start | bytes 786440 | tf_op jit(solution)/shard_map/ppermute | solution.py:347
  94.5 19.1 %collective-permute-start.15 = (bf16[2,256,256]{2,1,0:T(8,128)(2,1)S(1)}, bf16[2,256,256]{2,1,0:T(8,128)(2,1)S(1)}, u32[]{:S(2)}, u32[]{:S(2)}) collective-permute-start(bf16[2,256,256]{2,1,0:T(8,128)(2,1)S(1)} %join.10.refs_0_), channel_id=1, source_target_pairs={{0,2},{1,3},{2,0},{3,1},{4,6},{5,7},{6,4},{7,5},{8,10},{9,11},{10,... | collective-permute-start | bytes 786440 | tf_op jit(solution)/shard_map/ppermute | solution.py:347
  99.4 35.9 %collective-permute-start.25 = (bf16[2,256,256]{2,1,0:T(8,128)(2,1)S(1)}, bf16[2,256,256]{2,1,0:T(8,128)(2,1)S(1)}, u32[]{:S(2)}, u32[]{:S(2)}) collective-permute-start(bf16[2,256,256]{2,1,0:T(8,128)(2,1)S(1)} %join.12.refs_0_), channel_id=1, source_target_pairs={{0,8},{1,24},{2,0},{3,16},{4,12},{5,28},{6,4},{7,20},{8,9},{9,25},... | collective-permute-start | bytes 786440 | tf_op jit(solution)/shard_map/ppermute | solution.py:347
  101.8 33.5 %collective-permute-start.24 = (bf16[2,256,256]{2,1,0:T(8,128)(2,1)S(1)}, bf16[2,256,256]{2,1,0:T(8,128)(2,1)S(1)}, u32[]{:S(2)}, u32[]{:S(2)}) collective-permute-start(bf16[2,256,256]{2,1,0:T(8,128)(2,1)S(1)} %join.12.refs_0_), channel_id=1, source_target_pairs={{0,0},{1,16},{2,8},{3,24},{4,4},{5,20},{6,12},{7,28},{8,1},{9,17},... | collective-permute-start | bytes 786440 | tf_op jit(solution)/shard_map/ppermute | solution.py:347
  102.5 22.8 %collective-permute-start.9 = (bf16[2,256,256]{2,1,0:T(8,128)(2,1)S(1)}, bf16[2,256,256]{2,1,0:T(8,128)(2,1)S(1)}, u32[]{:S(2)}, u32[]{:S(2)}) collective-permute-start(bf16[2,256,256]{2,1,0:T(8,128)(2,1)S(1)} %join.8.refs_0_), channel_id=1, source_target_pairs={{0,8},{1,24},{2,0},{3,16},{4,12},{5,28},{6,4},{7,20},{8,9},{9,25},... | collective-permute-start | bytes 786440 | tf_op jit(solution)/shard_map/ppermute | solution.py:347
  112.0 38.0 %collective-permute-start.34 = (bf16[4,256,256]{2,1,0:T(8,128)(2,1)S(1)}, bf16[4,256,256]{2,1,0:T(8,128)(2,1)S(1)}, u32[]{:S(2)}, u32[]{:S(2)}) collective-permute-start(bf16[4,256,256]{2,1,0:T(8,128)(2,1)S(1)} %align.7.rest_0_), channel_id=1, source_target_pairs={{0,4},{1,5},{2,6},{3,7},{4,0},{5,1},{6,2},{7,3},{8,12},{9,13},{10,... | collective-permute-start | bytes 1572872 | tf_op jit(solution)/shard_map/ppermute | solution.py:347
  113.6 30.9 %collective-permute-start.8 = (bf16[2,256,256]{2,1,0:T(8,128)(2,1)S(1)}, bf16[2,256,256]{2,1,0:T(8,128)(2,1)S(1)}, u32[]{:S(2)}, u32[]{:S(2)}) collective-permute-start(bf16[2,256,256]{2,1,0:T(8,128)(2,1)S(1)} %join.8.refs_0_), channel_id=1, source_target_pairs={{0,0},{1,16},{2,8},{3,24},{4,4},{5,20},{6,12},{7,28},{8,1},{9,17},... | collective-permute-start | bytes 786440 | tf_op jit(solution)/shard_map/ppermute | solution.py:347
  125.3 16.7 %collective-permute-start.7 = (bf16[2,256,256]{2,1,0:T(8,128)(2,1)S(1)}, bf16[2,256,256]{2,1,0:T(8,128)(2,1)S(1)}, u32[]{:S(2)}, u32[]{:S(2)}) collective-permute-start(bf16[2,256,256]{2,1,0:T(8,128)(2,1)S(1)} %join.8.refs_0_), channel_id=1, source_target_pairs={{0,2},{1,3},{2,0},{3,1},{4,6},{5,7},{6,4},{7,5},{8,10},{9,11},{10,... | collective-permute-start | bytes 786440 | tf_op jit(solution)/shard_map/ppermute | solution.py:347
  135.3 11.8 %collective-permute-start.31 = (bf16[2,256,256]{2,1,0:T(8,128)(2,1)S(1)}, bf16[2,256,256]{2,1,0:T(8,128)(2,1)S(1)}, u32[]{:S(2)}, u32[]{:S(2)}) collective-permute-start(bf16[2,256,256]{2,1,0:T(8,128)(2,1)S(1)} %join.14.refs_0_), channel_id=1, source_target_pairs={{0,2},{1,3},{2,0},{3,1},{4,6},{5,7},{6,4},{7,5},{8,10},{9,11},{10,... | collective-permute-start | bytes 786440 | tf_op jit(solution)/shard_map/ppermute | solution.py:347
  135.3 14.6 %collective-permute-start.23 = (bf16[2,256,256]{2,1,0:T(8,128)(2,1)S(1)}, bf16[2,256,256]{2,1,0:T(8,128)(2,1)S(1)}, u32[]{:S(2)}, u32[]{:S(2)}) collective-permute-start(bf16[2,256,256]{2,1,0:T(8,128)(2,1)S(1)} %join.12.refs_0_), channel_id=1, source_target_pairs={{0,2},{1,3},{2,0},{3,1},{4,6},{5,7},{6,4},{7,5},{8,10},{9,11},{10,... | collective-permute-start | bytes 786440 | tf_op jit(solution)/shard_map/ppermute | solution.py:347
  142.0 14.8 %collective-permute-start.26 = (bf16[4,256,256]{2,1,0:T(8,128)(2,1)S(1)}, bf16[4,256,256]{2,1,0:T(8,128)(2,1)S(1)}, u32[]{:S(2)}, u32[]{:S(2)}) collective-permute-start(bf16[4,256,256]{2,1,0:T(8,128)(2,1)S(1)} %align.6.rest_0_), channel_id=1, source_target_pairs={{0,4},{1,5},{2,6},{3,7},{4,0},{5,1},{6,2},{7,3},{8,12},{9,13},{10,... | collective-permute-start | bytes 1572872 | tf_op jit(solution)/shard_map/ppermute | solution.py:347
  144.5 22.1 %collective-permute-start.18 = (bf16[4,256,256]{2,1,0:T(8,128)(2,1)S(1)}, bf16[4,256,256]{2,1,0:T(8,128)(2,1)S(1)}, u32[]{:S(2)}, u32[]{:S(2)}) collective-permute-start(bf16[4,256,256]{2,1,0:T(8,128)(2,1)S(1)} %align.5.rest_0_), channel_id=1, source_target_pairs={{0,4},{1,5},{2,6},{3,7},{4,0},{5,1},{6,2},{7,3},{8,12},{9,13},{10,... | collective-permute-start | bytes 1572872 | tf_op jit(solution)/shard_map/ppermute | solution.py:347
  147.1 30.1 %collective-permute-start.10 = (bf16[4,256,256]{2,1,0:T(8,128)(2,1)S(1)}, bf16[4,256,256]{2,1,0:T(8,128)(2,1)S(1)}, u32[]{:S(2)}, u32[]{:S(2)}) collective-permute-start(bf16[4,256,256]{2,1,0:T(8,128)(2,1)S(1)} %align.4.rest_0_), channel_id=1, source_target_pairs={{0,4},{1,5},{2,6},{3,7},{4,0},{5,1},{6,2},{7,3},{8,12},{9,13},{10,... | collective-permute-start | bytes 1572872 | tf_op jit(solution)/shard_map/ppermute | solution.py:347
